TPU v7x, 256 devices: a whole 4x4x8 slice. The times are simulated.
256 devices in a mesh: tm: 4 (over x), chan: 64 (over z, y, core).
Axes of the slice: x: 4, y: 4, z: 8, core: 2. Of those that a mesh axis runs over, the one named last changes fastest.
Arguments:
- voltages: bfloat16 [8, 4, 32768, 512], P(None, None, ('tm', 'chan')), may hold values from -6 to 6
- taps: float32 [4, 512], replicated, may hold values from -3 to 3
- busy_mask: int32 [512], replicated, may hold values from 0 to 1, as said below
- drift_low: int32 [512], replicated, may hold values from -16 to 1
Outputs:
- drift_power: float32 [8, 256, 16, 2048], P(None, 'chan', None, 'tm')
Inputs may be any that keep to these rules, and one draw needn't show every extreme that they name: `busy_mask`: exactly 256 entries are 1.
All inputs are finite; a program needn't handle non-finite values.
Results may differ from a plain program's by a relative error of at most 0.008.
Values may be sent and summed in bfloat16 or wider, within the bound.
No kernel may reach another device: no remote copies, remote signals or barrier semaphores. Data moves between devices by JAX's collectives and lax.ppermute only.
A program may use at most 128 MiB of HBM per device.

v0:
```python
import math

import jax
import jax.numpy as jnp
from jax import lax
from jax.sharding import PartitionSpec as P

FA = 32
FB = 64
TAPS = 4
NDRIFT = 16
DSPAN = 16
FSTEP = 4
CH_DEV = 1


def passed_along(block, axis, distance):
    devices = range(lax.axis_size(axis))
    route = [(i - distance, i) for i in devices if i - distance in devices]
    return lax.ppermute(block, axis, route)


def in_blocks(value, dim, devices):
    before, after = (value.shape[:dim], value.shape[dim + 1 :])
    return jnp.moveaxis(value.reshape(*before, devices, -1, *after), dim, 0)


def sum_at_owner(value, axis, dim):
    tiles = in_blocks(value, dim, lax.axis_size(axis))
    arrived = lax.all_to_all(tiles, axis, split_axis=0, concat_axis=0, tiled=True)
    return arrived.astype(jnp.float32).sum(axis=0)


def busy_index(busy_mask, busy_count):
    before = jnp.cumsum(busy_mask) - busy_mask
    slot_ids = jnp.arange(busy_count, dtype=jnp.int32)
    is_slot = (busy_mask[:, None] == 1) & (before[:, None] == slot_ids[None, :])
    positions = jnp.arange(busy_mask.shape[0], dtype=jnp.int32)
    return jnp.sum(jnp.where(is_slot, positions[:, None], 0), axis=0)


def real_dft(sample_pos, freq_ids, length):
    phase_index = sample_pos[:, None] * freq_ids[None, :] % length
    angles = phase_index.astype(jnp.float32) * (2.0 * math.pi / length)
    cosines = jnp.cos(angles)
    sine_table = jnp.sin(angles)
    upper = jnp.stack([cosines, -sine_table], axis=1)
    lower = jnp.stack([sine_table, cosines], axis=1)
    return jnp.stack([upper, lower], axis=0).astype(jnp.bfloat16)


def detect_power(spectra):
    items, lanes, chan_rows, samples = spectra.shape
    step_count = samples // (FA * FB)
    shaped = spectra.reshape(items, 2, 2, chan_rows, step_count, FA, FB)
    short_ids = jnp.arange(FA, dtype=jnp.int32)
    long_ids = jnp.arange(FB, dtype=jnp.int32)
    first_pass = jnp.einsum(
        "xopctab,paqf->xoqctfb",
        shaped,
        real_dft(short_ids, short_ids, FA),
        preferred_element_type=jnp.float32,
    )
    twist = short_ids[:, None] * long_ids[None, :] % (FA * FB)
    twist_angles = twist.astype(jnp.float32) * (2.0 * math.pi / (FA * FB))
    twist_cos = jnp.cos(twist_angles)
    twist_sin = jnp.sin(twist_angles)
    real_part = first_pass[:, :, 0]
    imag_part = first_pass[:, :, 1]
    turned = jnp.stack(
        [
            real_part * twist_cos + imag_part * twist_sin,
            imag_part * twist_cos - real_part * twist_sin,
        ],
        axis=2,
    ).astype(jnp.bfloat16)
    second_pass = jnp.einsum(
        "xoqctfb,qbsg->xosctgf",
        turned,
        real_dft(long_ids, long_ids, FB),
        preferred_element_type=jnp.float32,
    )
    powers = jnp.sum(second_pass * second_pass, axis=(1, 2)) / (4.0 * FA * FB)
    return powers.reshape(items, chan_rows, step_count, FA * FB)


def drift_rows(step_rows, first_step, drift_rates, first_bin, bin_width, pad_width):
    padded = jnp.pad(step_rows, ((0, 0), (0, 0), (0, 0), (pad_width, pad_width)))
    chan_rows = step_rows.shape[1]
    rate_count = drift_rates.shape[1]
    running = jnp.zeros((step_rows.shape[0], chan_rows, rate_count, bin_width), jnp.float32)
    for row_index in range(step_rows.shape[2]):
        step_time = first_step + row_index
        per_slot = []
        for slot_pos in range(chan_rows):
            power_row = padded[:, slot_pos, row_index]
            windows = []
            for rate_pos in range(rate_count):
                start = pad_width + first_bin + drift_rates[slot_pos, rate_pos] * step_time
                windows.append(lax.dynamic_slice_in_dim(power_row, start, bin_width, 1))
            per_slot.append(jnp.stack(windows, axis=1))
        running = running + jnp.stack(per_slot, axis=1)
    return running


def slot_rates(slot_part, drift_low):
    one_hot = slot_part[:, None] == jnp.arange(drift_low.shape[0], dtype=jnp.int32)[None, :]
    low_rates = jnp.sum(jnp.where(one_hot, drift_low[None, :], 0), axis=1)
    return low_rates[:, None] + jnp.arange(NDRIFT, dtype=jnp.int32)[None, :]


def shards(voltages, taps, busy_mask, drift_low):
    tm_count = lax.axis_size("tm")
    chan_devices = lax.axis_size("chan")
    count_of_beams, lanes, spec_dev, chan_count = voltages.shape
    busy_count = CH_DEV * tm_count * chan_devices
    step_count = FSTEP * tm_count
    pad_width = DSPAN * (step_count - 1)
    slot_index = busy_index(busy_mask, busy_count)
    coarse_dft = real_dft(jnp.arange(chan_count, dtype=jnp.int32), slot_index, chan_count)
    following = passed_along(voltages[:, :, : TAPS - 1], ("tm", "chan"), -1)
    extended = jnp.concatenate([voltages, following], axis=2)
    filtered = taps[0] * extended[:, :, 0:spec_dev]
    for tap_index in range(1, TAPS):
        filtered = filtered + taps[tap_index] * extended[:, :, tap_index : tap_index + spec_dev]
    filtered = filtered.astype(jnp.bfloat16).reshape(count_of_beams, 2, 2, spec_dev, chan_count)
    coarse = jnp.einsum(
        "bopsn,pnqr->boqrs", filtered, coarse_dft, preferred_element_type=jnp.float32
    )
    coarse = (
        (coarse * chan_count ** (-0.5))
        .astype(jnp.bfloat16)
        .reshape(count_of_beams, 4, busy_count, spec_dev)
    )
    powers = detect_power(lax.all_to_all(coarse, "chan", split_axis=2, concat_axis=3, tiled=True))
    slot_count = CH_DEV * tm_count
    drift_rates = slot_rates(
        lax.dynamic_slice_in_dim(slot_index, lax.axis_index("chan") * slot_count, slot_count),
        drift_low,
    )
    first_step = lax.axis_index("tm") * FSTEP
    partial_value = drift_rows(powers, first_step, drift_rates, 0, FA * FB, pad_width)
    summed = sum_at_owner(partial_value.astype(jnp.bfloat16), "tm", 3)
    result = summed / step_count
    return result


def solution(mesh):
    in_specs = (P(None, None, ("tm", "chan"), None), P(), P(), P())
    out_specs = P(None, "chan", None, "tm")
    return jax.shard_map(shards, mesh=mesh, in_specs=in_specs, out_specs=out_specs, check_vma=False)
```

profile of v0, /device:TPU:32, one launch (start us, length us, event | category | flops | bytes accessed | tf_op | source)
XLA Modules:
  0.0 274.5 jit_solution(3093850198219904586)
XLA Ops:
  0.0 1.0 slice.191
  1.0 0.0 copy-start.1
  1.0 0.0 copy-start.2
  1.0 3.9 %collective-permute-start = (bf16[8,4,3,512]{3,2,1,0:T(4,128)(2,1)S(1)}, bf16[8,4,3,512]{3,2,1,0:T(4,128)(2,1)S(1)}, u32[]{:S(2)}, u32[]{:S(2)}) collective-permute-start(bf16[8,4,3,512]{3,2,1,0:T(4,128)(2,1)S(1)} %slice.191), channel_id=1, source_target_pairs={{1,0},{2,1},{3,2},{4,3},{5,4},{6,5},{7,6},{8,7},{9,8},{10,9},{11,1... | collective-permute-start | bytes 294920 | tf_op jit(solution)/shard_map/ppermute | solution.py:20
  4.9 4.6 %constant_dynamic-update-slice_fusion.1 = bf16[8,4,131,512]{3,2,1,0:T(8,128)(2,1)} fusion(bf16[8,4,128,512]{3,2,1,0:T(8,128)(2,1)} %param.4), kind=kLoop, calls=%fused_computation.47 | loop fusion | bytes 8388608
  9.5 0.3 reduce-window.9
  9.8 0.1 slice.187
  9.9 0.1 slice_reduce_fusion
  10.1 0.1 bitcast_subtract_fusion
  10.2 0.2 select_reduce_fusion
  10.4 2.5 negate_convert_fusion
  12.9 0.1 maximum_bitcast_fusion.2
  13.0 0.0 collective-permute-done
  13.0 0.7 constant_dynamic-update-slice_fusion
  13.7 10.8 %add_convert_fusion = bf16[8,4,128,512]{3,2,1,0:T(8,128)(2,1)S(1)} fusion(bf16[8,4,128,512]{3,2,1,0:T(8,128)(2,1)} %param.4, bf16[8,4,131,512]{3,2,1,0:T(8,128)(2,1)} %constant_dynamic-update-slice_fusion, f32[512]{0:T(512)S(1)} %bitcast.671, f32[512]{0:T(512)S(1)} %bitcast.672, f32[512]{0:T(512)S(1)} %bitcast.670, f32[512]{0:T(512)S(1)} %bitcast.669), kind=kLoop, calls=%fused_computation.2 | loop fusion | flops 25165824 | bytes 20979712 | tf_op jit(solution)/shard_map/convert_element_type | solution.py:126
  24.5 2.7 fusion.17
  27.2 0.1 copy.30
  27.3 0.0 copy-start.3
  27.3 3.0 %copy.31 = bf16[8,4,256,128]{3,1,0,2:T(4,128)(2,1)} copy(bf16[8,4,256,128]{3,2,1,0:T(8,128)(2,1)S(1)} %bitcast.410) | data formatting | bytes 4194304 | tf_op jit(solution)/shard_map/reshape | solution.py:133
  30.3 9.9 %all-to-all-start = ((bf16[8,4,256,128]{3,1,0,2:T(4,128)(2,1)}), bf16[8,4,256,128]{3,1,0,2:T(4,128)(2,1)S(1)}, u32[]{:S(2)}, u32[]{:S(2)}) async-start(bf16[8,4,256,128]{3,1,0,2:T(4,128)(2,1)} %copy.31), calls=%async_computation | async-start | bytes 4194304 | tf_op jit(solution)/shard_map/all_to_all | solution.py:135
  40.2 0.1 dynamic_slice.771
  40.3 0.2 select_reduce_fusion.1
  40.5 0.1 iota_add_fusion
  40.5 0.7 fusion.64
  58.7 0.7 fusion.63
  107.0 0.7 fusion.61
  155.3 0.7 fusion.62
  206.8 0.1 fusion.56
  206.9 0.1 fusion.50
  207.0 0.1 negate_convert_fusion.2
  207.1 0.1 fusion.53
  207.2 0.2 negate_convert_fusion.1
  207.4 0.0 all-to-all-done
  207.4 1.3 copy-done
  208.8 2.9 %copy.58 = bf16[8,4,64,4,128]{4,2,3,1,0:T(8,128)(2,1)S(1)} copy(bf16[8,4,64,4,128]{4,1,0,3,2:T(4,128)(2,1)} %bitcast.409) | data formatting | bytes 4194304 | tf_op jit(solution)/shard_map/all_to_all | solution.py:135
  211.7 3.3 %reshape.1398 = bf16[8,2,2,4,4,32,64]{6,5,4,3,2,1,0:T(8,128)(2,1)} reshape(bf16[8,4,4,64,128]{4,3,2,1,0:T(8,128)(2,1)S(1)} %bitcast.408) | data formatting | bytes 4194304 | tf_op jit(solution)/shard_map/reshape | solution.py:55
  215.0 3.5 %fusion.11 = f32[8,2,2,4,4,32,64]{6,5,4,3,1,0,2:T(8,128)S(1)} fusion(bf16[8,2,2,4,4,32,64]{6,5,4,3,2,1,0:T(8,128)(2,1)} %reshape.1398, bf16[1,32,2,32]{1,3,0,2:T(8,128)(2,1)S(1)} %get-tuple-element.284, bf16[1,32,2,32]{1,3,0,2:T(8,128)(2,1)S(1)} %get-tuple-element.283), kind=kOutput, calls=%fused_computation.19 | convolution fusion | flops 134234112 | bytes 6299648 | tf_op jit(solution)/shard_map/xopctab,paqf->xoqctfb/dot_general | solution.py:58
  218.5 1.2 add_convert_fusion.1
  219.7 2.3 fusion
  222.0 0.2 multiply_bitcast_fusion
  222.3 2.8 %copy.35 = f32[8,4,4,64,32]{4,3,0,2,1:T(8,128)} copy(f32[8,4,4,64,32]{3,4,2,1,0:T(8,128)S(1)} %multiply_bitcast_fusion) | data formatting | bytes 2097152 | tf_op jit(solution)/shard_map/div | solution.py:83
  225.0 3.9 %div.19 = f32[8,4,4,2048]{3,0,2,1:T(8,128)S(1)} reshape(f32[8,4,4,64,32]{4,3,0,2,1:T(8,128)} %copy.35) | data formatting | bytes 2097152 | tf_op jit(solution)/shard_map/div | solution.py:83
  228.9 0.4 pad_slice_fusion.15
  229.3 0.4 constant_dynamic-slice_fusion
  229.7 0.4 constant_dynamic-slice_fusion.16
  230.1 0.4 constant_dynamic-slice_fusion.32
  230.6 0.4 constant_dynamic-slice_fusion.48
  231.0 0.4 constant_dynamic-slice_fusion.64
  231.4 0.4 constant_dynamic-slice_fusion.80
  231.9 0.4 constant_dynamic-slice_fusion.96
  232.3 0.4 constant_dynamic-slice_fusion.112
  232.8 0.4 constant_dynamic-slice_fusion.128
  233.2 0.4 constant_dynamic-slice_fusion.144
  233.6 0.4 constant_dynamic-slice_fusion.160
  234.1 0.4 constant_dynamic-slice_fusion.176
  234.5 0.4 constant_dynamic-slice_fusion.192
  235.0 0.4 constant_dynamic-slice_fusion.208
  235.4 0.4 constant_dynamic-slice_fusion.224
  235.8 0.4 constant_dynamic-slice_fusion.240
  239.9 1.7 fusion.16
  241.6 30.9 %all_to_all.20 = bf16[4,8,4,16,512]{4,1,3,2,0:T(8,128)(2,1)S(1)} all-to-all(bf16[4,8,4,16,512]{4,1,3,2,0:T(8,128)(2,1)S(1)} %fusion.16), channel_id=1, replica_groups=mesh['tm'=4,'chan'=64] {'tm'}, dimensions={0} | all-to-all | bytes 4194304 | tf_op jit(solution)/shard_map/all_to_all | solution.py:30
  272.5 0.3 convert_reduce_fusion
  272.8 0.1 broadcast_multiply_fusion
  272.9 1.6 copy.37
  (265 shorter events, 2.0 us)
Async XLA Ops:
  1.0 8.5 %copy-start.1 = (s32[512]{0:T(512)S(1)}, s32[512]{0:T(512)}, u32[]{:S(2)}) copy-start(s32[512]{0:T(512)} %param.6) | copy-start | bytes 6148
  1.0 9.1 %copy-start.2 = (f32[4,512]{1,0:T(4,128)S(1)}, f32[4,512]{1,0:T(4,128)}, u32[]{:S(2)}) copy-start(f32[4,512]{1,0:T(4,128)} %param.5) | copy-start | bytes 24580
  1.0 11.9 %collective-permute-start = (bf16[8,4,3,512]{3,2,1,0:T(4,128)(2,1)S(1)}, bf16[8,4,3,512]{3,2,1,0:T(4,128)(2,1)S(1)}, u32[]{:S(2)}, u32[]{:S(2)}) collective-permute-start(bf16[8,4,3,512]{3,2,1,0:T(4,128)(2,1)S(1)} %slice.191), channel_id=1, source_target_pairs={{1,0},{2,1},{3,2},{4,3},{5,4},{6,5},{7,6},{8,7},{9,8},{10,9},{11,1... | collective-permute-start | bytes 294920 | tf_op jit(solution)/shard_map/ppermute | solution.py:20
  27.3 12.9 %copy-start.3 = (s32[512]{0:T(512)S(1)}, s32[512]{0:T(512)}, u32[]{:S(2)}) copy-start(s32[512]{0:T(512)} %param.7) | copy-start | bytes 6148
  30.3 177.1 %all-to-all-start = ((bf16[8,4,256,128]{3,1,0,2:T(4,128)(2,1)}), bf16[8,4,256,128]{3,1,0,2:T(4,128)(2,1)S(1)}, u32[]{:S(2)}, u32[]{:S(2)}) async-start(bf16[8,4,256,128]{3,1,0,2:T(4,128)(2,1)} %copy.31), calls=%async_computation | async-start | bytes 4194304 | tf_op jit(solution)/shard_map/all_to_all | solution.py:135
  207.4 1.3 copy-start
where the time goes:
time: 277 us; the launch traced here: 274 us
  between operations  166 us (60%)
  local copies, waits for them, and re-layouts  37.3 us (13%)
  blocking collectives  30.9 us (11%)
  other arithmetic  18.4 us (7%)
  starting transfers between devices  13.8 us (5%)
  matrix products  8.46 us (3%)
    all_to_all x1, blocking collectives, sum_at_owner(): lax.all_to_all(tiles, axis, split_axis=0, concat_axis=0, tiled=True)  30.9 us
    convert_element_type x1, other arithmetic, shards(): filtered.astype(jnp.bfloat16)  10.8 us
    all_to_all x1, starting transfers between devices, shards(): lax.all_to_all(coarse, 'chan', split_axis=2, concat_axis=3, tiled=True)  9.89 us
    unnamed x249, local copies, waits for them, and re-layouts  7.68 us
    dynamic_slice x16, local copies, waits for them, and re-layouts, drift_rows(): windows.append(lax.dynamic_slice_in_dim(power_row, start, bin_width, 1))  6.74 us
    div x2, local copies, waits for them, and re-layouts, detect_power(): powers = jnp.sum(second_pass * second_pass, axis=(1, 2)) / (4.0 * FA * FB)  6.61 us
  transfers between devices with their start and end apart: 2, of which 0 were waited for; matrix products, arithmetic and copies ran while one was open for 4% of the time, Pallas kernels for 0%

commit v1 on v0

v1 whole, which is shorter than its diff:
```python
import math

import jax
import jax.numpy as jnp
import numpy as np
from jax import lax
from jax.experimental import pallas as pl
from jax.experimental.pallas import tpu as pltpu
from jax.sharding import Mesh, PartitionSpec as P

TAPS = 4
NDRIFT = 16
N = 512
FINE = 2048
BEAMS = 8
STEPS = 16
BLK = 128
GRP = 16
PAD = 256
WIN = 1024
BINS = 512
f32 = jnp.float32
bf16 = jnp.bfloat16


def np_bf16(a):
    return np.asarray(a, np.float32).astype(jnp.bfloat16)


def coarse_tables():
    idx = np.arange(N)
    ang = (idx[:, None] * idx[None, :]) % N * (2.0 * math.pi / N)
    return np_bf16(np.cos(ang)), np_bf16(np.sin(ang))


def fine_tables():
    f1 = np.arange(GRP)
    j = np.arange(BLK)
    ang = (f1[:, None] * j[None, :]) % FINE * (2.0 * math.pi / FINE)
    tw = np.stack([np.cos(ang), np.sin(ang)]).astype(np.float32)
    a2 = (j[:, None] * j[None, :]) % BLK * (2.0 * math.pi / BLK)
    c, s = np.cos(a2), np.sin(a2)
    dft = np.concatenate([np.concatenate([c, -s], 1), np.concatenate([s, c], 1)], 0)
    src = np.arange(256)
    perm = np.zeros((256, 256), np.float32)
    perm[src, src // 16 + 16 * (src % 16)] = 1.0
    return tw, np_bf16(dft), np_bf16(perm)


def coarse_kernel(v_ref, halo_ref, taps_ref, mask_ref, cos_ref, sin_ref, out_ref, wt_ref, filt_ref):
    @pl.when(pl.program_id(0) == 0)
    def _():
        row = lax.broadcasted_iota(jnp.int32, (N, N), 0)
        col = lax.broadcasted_iota(jnp.int32, (N, N), 1)
        upper = (row < col).astype(f32).astype(bf16)
        mask = jnp.broadcast_to(mask_ref[...], (8, N))
        before = jnp.dot(mask.astype(f32).astype(bf16), upper, preferred_element_type=f32)[0:1]
        rp = lax.broadcasted_iota(jnp.int32, (256, N), 0)
        g = rp // 16
        zh = (rp // 4) % 4
        i = rp % 4
        slot = zh * 64 + g * 4 + i
        hit = (before.astype(jnp.int32) == slot) & (mask_ref[...] == 1)
        one_hot = hit.astype(f32).astype(bf16)
        c = jnp.dot(one_hot, cos_ref[...], preferred_element_type=f32)
        s = jnp.dot(one_hot, sin_ref[...], preferred_element_type=f32)
        cb = c.astype(bf16).reshape(GRP, 16, N)
        sb = s.astype(bf16).reshape(GRP, 16, N)
        nb = (-s).astype(bf16).reshape(GRP, 16, N)
        wt_ref[:, 0:16, 0:N] = cb
        wt_ref[:, 0:16, N : 2 * N] = sb
        wt_ref[:, 16:32, 0:N] = nb
        wt_ref[:, 16:32, N : 2 * N] = cb

    for o in range(2):
        for p in range(2):
            for c in range(N // 128):
                lanes = pl.ds(c * 128, 128)
                main = v_ref[0, 2 * o + p, :, lanes].astype(f32)
                tail = halo_ref[0, 2 * o + p, :, lanes].astype(f32)
                ext = jnp.concatenate([main, tail], axis=0)
                acc = taps_ref[0:1, lanes] * main
                for tap in range(1, TAPS):
                    acc = acc + taps_ref[tap : tap + 1, lanes] * ext[tap : tap + BLK]
                filt_ref[pl.ds(o * BLK, BLK), pl.ds(p * N + c * 128, 128)] = acc.astype(bf16)
    res = lax.dot_general(
        wt_ref[...].reshape(2 * 256, 2 * N),
        filt_ref[...],
        (((1,), (1,)), ((), ())),
        preferred_element_type=f32,
    )
    res = (res * (N ** -0.5)).astype(bf16)
    out_ref[...] = res.reshape(GRP, 1, 32, 256)


def coarse(volt, halo, taps, mask, cos_t, sin_t):
    return pl.pallas_call(
        coarse_kernel,
        grid=(BEAMS,),
        in_specs=[
            pl.BlockSpec((1, 4, BLK, N), lambda b: (b, 0, 0, 0)),
            pl.BlockSpec((1, 4, 8, N), lambda b: (b, 0, 0, 0)),
            pl.BlockSpec((TAPS, N), lambda b: (0, 0)),
            pl.BlockSpec((1, N), lambda b: (0, 0)),
            pl.BlockSpec((N, N), lambda b: (0, 0)),
            pl.BlockSpec((N, N), lambda b: (0, 0)),
        ],
        out_specs=pl.BlockSpec((GRP, 1, 32, 256), lambda b: (0, b, 0, 0)),
        out_shape=jax.ShapeDtypeStruct((GRP, BEAMS, 32, 256), bf16),
        scratch_shapes=[pltpu.VMEM((GRP, 32, 2 * N), bf16), pltpu.VMEM((256, 2 * N), bf16)],
        name="coarse",
    )(volt, halo, taps, mask, cos_t, sin_t)


def dft4(x):
    (r0, i0), (r1, i1), (r2, i2), (r3, i3) = x
    ar, ai = r0 + r2, i0 + i2
    br, bi = r0 - r2, i0 - i2
    cr, ci = r1 + r3, i1 + i3
    dr, di = r1 - r3, i1 - i3
    return [(ar + cr, ai + ci), (br + di, bi - dr), (ar - cr, ai - ci), (br - di, bi + dr)]


def turn(x, cos, sin):
    r, i = x
    return r * cos + i * sin, i * cos - r * sin


def fine_kernel(x_ref, tw_ref, dft_ref, perm_ref, out_ref, lhs_ref, pow_ref):
    b = pl.program_id(0)

    @pl.when(b == 0)
    def _():
        pow_ref[:, 0:2, :] = jnp.zeros((128, 2, 128), f32)
        pow_ref[:, 18:20, :] = jnp.zeros((128, 2, 128), f32)

    total = None
    for o in range(2):
        lanes = pl.ds(o * BLK, BLK)
        stage = []
        for m in range(4):
            x = []
            for a in range(4):
                k = 4 * a + m
                x.append((x_ref[k, 0, 0:16, lanes].astype(f32), x_ref[k, 0, 16:32, lanes].astype(f32)))
            y = dft4(x)
            row = []
            for c in range(4):
                if m * c == 0:
                    row.append(y[c])
                else:
                    ang = 2.0 * math.pi * m * c / 16.0
                    row.append(turn(y[c], math.cos(ang), math.sin(ang)))
            stage.append(row)
        for c in range(4):
            y = dft4([stage[m][c] for m in range(4)])
            for d in range(4):
                f1 = c + 4 * d
                if f1 == 0:
                    r, i = y[d]
                else:
                    r, i = turn(y[d], tw_ref[0, f1 : f1 + 1, :], tw_ref[1, f1 : f1 + 1, :])
                lhs_ref[o, f1 * 16 : (f1 + 1) * 16, 0:BLK] = r.astype(bf16)
                lhs_ref[o, f1 * 16 : (f1 + 1) * 16, BLK : 2 * BLK] = i.astype(bf16)
        z = jnp.dot(lhs_ref[o], dft_ref[...], preferred_element_type=f32)
        part = z[:, 0:BLK] * z[:, 0:BLK] + z[:, BLK : 2 * BLK] * z[:, BLK : 2 * BLK]
        total = part if total is None else total + part
    total = total * (1.0 / 8192.0)
    lane = lax.broadcasted_iota(jnp.int32, (16, 128), 1)
    rows = [[None, None] for _ in range(8)]
    for h in range(2):
        v = [total[(8 * h + i) * 16 : (8 * h + i + 1) * 16] for i in range(8)]
        for dist in (4, 2, 1):
            low = (lane // 16) % (2 * dist) < dist
            new = list(v)
            for i in range(8):
                if i & dist == 0:
                    a, e = v[i], v[i + dist]
                    new[i] = jnp.where(low, a, pltpu.roll(e, dist * 16, 1))
                    new[i + dist] = jnp.where(low, pltpu.roll(a, 128 - dist * 16, 1), e)
            v = new
        for m in range(8):
            rows[m][h] = v[m]
    mixed = jnp.concatenate([jnp.concatenate(rows[m], axis=1) for m in range(8)], axis=0).astype(bf16)
    q = jnp.dot(mixed, perm_ref[...], preferred_element_type=f32)
    for m in range(8):
        for h in range(2):
            pow_ref[pl.ds(b, 16, stride=8), 2 + 2 * m + h, :] = q[m * 16 : (m + 1) * 16, h * 128 : (h + 1) * 128]

    @pl.when(b == BEAMS - 1)
    def _():
        for x in range(4):
            for w in range(WIN // 128):
                out_ref[x, :, w * 128 : (w + 1) * 128] = pow_ref[:, 4 * x + w, :].astype(bf16)


def fine(x, tw, dft, perm):
    return pl.pallas_call(
        fine_kernel,
        grid=(BEAMS,),
        in_specs=[
            pl.BlockSpec((GRP, 1, 32, 256), lambda b: (0, b, 0, 0)),
            pl.BlockSpec((2, GRP, BLK), lambda b: (0, 0, 0)),
            pl.BlockSpec((256, 256), lambda b: (0, 0)),
            pl.BlockSpec((256, 256), lambda b: (0, 0)),
        ],
        out_specs=pl.BlockSpec((4, 128, WIN), lambda b: (0, 0, 0)),
        out_shape=jax.ShapeDtypeStruct((4, 128, WIN), bf16),
        scratch_shapes=[pltpu.VMEM((2, 256, 256), bf16), pltpu.VMEM((128, 20, 128), f32)],
        name="fine",
    )(x, tw, dft, perm)


def drift_kernel(low_ref, x_ref, out_ref, wide_ref):
    for t in range(STEPS):
        for w in range(WIN // 128):
            wide_ref[t, w] = x_ref[t, :, w * 128 : (w + 1) * 128].astype(f32)
    lane = lax.broadcasted_iota(jnp.int32, (8, 128), 1)

    def body(ij, carry):
        i = ij // NDRIFT
        j = ij % NDRIFT
        d = low_ref[i] + j
        rows = pl.ds(pl.multiple_of(i * 8, 8), 8)
        acc = [None] * 4
        for t in range(STEPS):
            start = PAD + d * t
            base = start // 128
            off = start % 128
            if t == 0:
                w = [wide_ref[t, 2 + k, rows, :] for k in range(4)]
            else:
                r = [pltpu.roll(wide_ref[t, base + k, rows, :], (128 - off) % 128, 1) for k in range(5)]
                keep = lane < 128 - off
                w = [jnp.where(keep, r[k], r[k + 1]) for k in range(4)]
            acc = w if t == 0 else [acc[k] + w[k] for k in range(4)]
        for k in range(4):
            out_ref[pl.ds(i * NDRIFT + j, 8, stride=64), k, :] = acc[k] * (1.0 / STEPS)
        return carry

    lax.fori_loop(0, 4 * NDRIFT, body, 0)


def drift(low, x):
    return pl.pallas_call(
        drift_kernel,
        in_specs=[
            pl.BlockSpec(memory_space=pltpu.SMEM),
            pl.BlockSpec(memory_space=pltpu.VMEM),
        ],
        out_specs=pl.BlockSpec(memory_space=pltpu.VMEM),
        out_shape=jax.ShapeDtypeStruct((BEAMS * 64, 4, 128), f32),
        scratch_shapes=[pltpu.VMEM((STEPS, WIN // 128, 32, 128), f32)],
        name="drift",
    )(low, x)


def own_low_rates(busy_mask, drift_low, first):
    before = jnp.cumsum(busy_mask) - busy_mask
    slots = first + jnp.arange(4, dtype=jnp.int32)
    hit = (busy_mask[None, :] == 1) & (before[None, :] == slots[:, None])
    return jnp.sum(jnp.where(hit, drift_low[None, :], 0), axis=1).astype(jnp.int32)


def shards(voltages, taps, busy_mask, drift_low):
    axes = ("x", "zh", "zl", "y", "core")
    devices = lax.axis_size(axes)
    head = lax.slice_in_dim(voltages, 0, 8, axis=2)
    halo = lax.ppermute(head, axes, [(i + 1, i) for i in range(devices - 1)])
    cos_t, sin_t = coarse_tables()
    tw, dft, perm = fine_tables()
    blocks = coarse(voltages, halo, taps, busy_mask.reshape(1, N), jnp.asarray(cos_t), jnp.asarray(sin_t))
    times = lax.all_to_all(blocks, ("zl", "y", "core"), split_axis=0, concat_axis=0, tiled=True)
    powers = fine(times, jnp.asarray(tw), jnp.asarray(dft), jnp.asarray(perm))
    wins = lax.all_to_all(powers.reshape(16, 32, WIN), ("x", "zh"), split_axis=0, concat_axis=0, tiled=True)
    low = own_low_rates(busy_mask, drift_low, lax.axis_index(("zh", "zl", "y", "core")) * 4)
    out = drift(low, wins)
    return out.reshape(BEAMS, 4, NDRIFT, BINS)


def solution(mesh):
    fold = Mesh(mesh.devices.reshape(4, 4, 2, 4, 2), ("x", "zh", "zl", "y", "core"))
    chan = ("zh", "zl", "y", "core")
    in_specs = (P(None, None, ("x",) + chan, None), P(), P(), P())
    out_specs = P(None, chan, None, "x")
    return jax.shard_map(shards, mesh=fold, in_specs=in_specs, out_specs=out_specs, check_vma=False)
```

time: 277 us -> 128 us (0.46)
  between operations: 166 us -> 0.05 us
  Pallas kernels: 0 us -> 38.8 us
  waiting for transfers between devices: 0.01 us -> 32.3 us
  local copies, waits for them, and re-layouts: 37.3 us -> 5.45 us
  other arithmetic: 18.4 us -> 1.2 us
  matrix products: 8.46 us -> 0 us
    pallas_call x0 -> x3, Pallas kernels: none -> 38.8 us  [the longest x1 16.9 us: drift(): pl.pallas_call(drift_kernel, in_specs=[pl.BlockSpec(memory_space=pltpu.SM...]
    all_to_all x1, waiting for transfers between devices: 0.01 us -> 28.4 us  [shards(): lax.all_to_all(powers.reshape(16, 32, WIN), ('x', 'zh'), split_axis=0, co...]
    convert_element_type x1 -> x0, other arithmetic: 10.8 us -> none  [shards(): filtered.astype(jnp.bfloat16)]
    dot_general x3 -> x0, matrix products: 8.46 us -> none  [the longest x1 3.48 us: detect_power(): jnp.einsum('xopctab,paqf->xoqctfb', shaped, real_dft(short_ids, short_ids...]
    div x3 -> x0, local copies, waits for them, and re-layouts: 8.19 us -> none  [the longest x2 6.61 us: detect_power(): powers = jnp.sum(second_pass * second_pass, axis=(1, 2)) / (4.0 * FA * FB)]
    dynamic_slice x17 -> x0, local copies, waits for them, and re-layouts: 6.81 us -> none  [the longest x16 6.74 us: drift_rows(): windows.append(lax.dynamic_slice_in_dim(power_row, start, bin_width, 1))]
    unnamed x249 -> x8, local copies, waits for them, and re-layouts: 7.68 us -> 1.68 us
    another operation x11 -> x2, other arithmetic: 4.62 us -> 0.34 us
  transfers between devices with their start and end apart: 2 -> 2, of which waited for: 0 -> 2; matrix products, arithmetic and copies ran while one was open for 4% -> 1% of each run, Pallas kernels for 0% -> 0%
where the time goes in v1:
time: 128 us; the launch traced here: 127 us
  Pallas kernels  38.8 us (30%)
  blocking collectives  33.6 us (26%)
  waiting for transfers between devices  32.3 us (25%)
  starting transfers between devices  15.3 us (12%)
  local copies, waits for them, and re-layouts  5.45 us (4%)
    all_to_all x1, blocking collectives, shards(): lax.all_to_all(blocks, ('zl', 'y', 'core'), split_axis=0, concat_axis=0,...  33.6 us
    all_to_all x1, waiting for transfers between devices, shards(): lax.all_to_all(powers.reshape(16, 32, WIN), ('x', 'zh'), split_axis=0, co...  28.4 us
    pallas_call x1, Pallas kernels, drift(): pl.pallas_call(drift_kernel, in_specs=[pl.BlockSpec(memory_space=pltpu.SM...  16.9 us
    all_to_all x1, starting transfers between devices, shards(): lax.all_to_all(powers.reshape(16, 32, WIN), ('x', 'zh'), split_axis=0, co...  11.4 us
    pallas_call x1, Pallas kernels, coarse(): pl.pallas_call(coarse_kernel, grid=(BEAMS,), in_specs=[pl.BlockSpec((1, 4...  10.9 us
    pallas_call x1, Pallas kernels, fine(): pl.pallas_call(fine_kernel, grid=(BEAMS,), in_specs=[pl.BlockSpec((GRP, 1...  10.9 us
    ppermute x1, starting transfers between devices, shards(): halo = lax.ppermute(head, axes, [(i + 1, i) for i in range(devices - 1)])  3.91 us
    ppermute x1, waiting for transfers between devices, shards(): halo = lax.ppermute(head, axes, [(i + 1, i) for i in range(devices - 1)])  3.87 us
  transfers between devices with their start and end apart: 2, of which 2 were waited for; matrix products, arithmetic and copies ran while one was open for 1% of the time, Pallas kernels for 0%

profile of v1, /device:TPU:32, one launch (start us, length us, event | category | flops | bytes accessed | tf_op | source)
XLA Modules:
  0.0 126.6 jit_solution(10755437079630044122)
XLA Ops:
  0.0 1.0 slice.12
  1.0 3.9 %collective-permute-start = (bf16[8,4,8,512]{3,2,1,0:T(8,128)(2,1)S(1)}, bf16[8,4,8,512]{3,2,1,0:T(8,128)(2,1)S(1)}, u32[]{:S(2)}, u32[]{:S(2)}) collective-permute-start(bf16[8,4,8,512]{3,2,1,0:T(8,128)(2,1)S(1)} %slice.12), channel_id=1, source_target_pairs={{1,0},{2,1},{3,2},{4,3},{5,4},{6,5},{7,6},{8,7},{9,8},{10,9},{11,1... | collective-permute-start | bytes 786440 | tf_op jit(solution)/shard_map/ppermute | solution.py:269
  4.9 3.9 %collective-permute-done.halo_ref = bf16[8,4,8,512]{3,2,1,0:T(8,128)(2,1)S(1)} collective-permute-done((bf16[8,4,8,512]{3,2,1,0:T(8,128)(2,1)S(1)}, bf16[8,4,8,512]{3,2,1,0:T(8,128)(2,1)S(1)}, u32[]{:S(2)}, u32[]{:S(2)}) %collective-permute-start) | collective-permute-done | bytes 262176 | tf_op jit(solution)/shard_map/ppermute | solution.py:269
  8.8 0.0 copy-start.1
  8.8 0.7 copy-done.1
  9.5 10.9 %coarse.1 = bf16[16,8,32,256]{3,2,1,0:T(8,128)(2,1)} custom-call(bf16[8,4,128,512]{3,2,1,0:T(8,128)(2,1)} %v_ref.1, bf16[8,4,8,512]{3,2,1,0:T(8,128)(2,1)} %copy-done.1, f32[4,512]{1,0:T(4,128)} %taps_ref.1, s32[1,512]{1,0:T(1,128)} %bitcast.6, bf16[512,512]{1,0:T(8,128)(2,1)} %constant.40.clone.cos_ref, bf16[512,512]{1,0:T(8,128)(2,1)} %constant.41.clone.sin_ref), custom_call_target="tpu_custom_call" | custom-call | tf_op jit(solution)/shard_map/coarse/pallas_call | solution.py:97
  20.4 33.6 %all_to_all.10.x_ref = bf16[16,8,32,256]{3,2,1,0:T(8,128)(2,1)} all-to-all(bf16[16,8,32,256]{3,2,1,0:T(8,128)(2,1)} %coarse.1), channel_id=1, replica_groups=mesh['x'=4,'zh'=4,'zl'=2,'y'=4,'core'=2] {'zl','y','core'}, dimensions={0} | all-to-all | bytes 4194304 | tf_op jit(solution)/shard_map/all_to_all | solution.py:273
  54.0 0.0 copy-start.2
  54.0 0.0 copy-start.3
  54.0 10.9 %fine.1 = bf16[4,128,1024]{2,1,0:T(8,128)(2,1)} custom-call(bf16[16,8,32,256]{3,2,1,0:T(8,128)(2,1)} %all_to_all.10.x_ref, f32[2,16,128]{2,1,0:T(8,128)} %constant.42.clone.tw_ref, bf16[256,256]{1,0:T(8,128)(2,1)} %constant.43.clone.dft_ref, bf16[256,256]{1,0:T(8,128)(2,1)} %constant.44.clone.perm_ref), custom_call_target="tpu_custom_call" | custom-call | tf_op jit(solution)/shard_map/fine/pallas_call | solution.py:198
  64.9 11.4 %all-to-all-start.1 = ((bf16[16,32,1024]{2,1,0:T(8,128)(2,1)}), bf16[16,32,1024]{2,1,0:T(8,128)(2,1)S(1)}, u32[]{:S(2)}, u32[]{:S(2)}) async-start(bf16[16,32,1024]{2,1,0:T(8,128)(2,1)} %bitcast.5), calls=%async_computation.1 | async-start | bytes 2097152 | tf_op jit(solution)/shard_map/all_to_all | solution.py:275
  76.3 0.0 copy-done.2
  76.3 0.3 reduce-window.9
  76.6 0.1 slice.10
  76.7 0.1 slice_reduce_fusion
  76.8 0.1 bitcast_subtract_fusion
  76.9 0.0 copy-done.3
  76.9 0.8 select_reduce_fusion.low_ref
  77.7 28.4 %all-to-all-done.1.x_ref = bf16[16,32,1024]{2,1,0:T(8,128)(2,1)S(1)} async-done(((bf16[16,32,1024]{2,1,0:T(8,128)(2,1)}), bf16[16,32,1024]{2,1,0:T(8,128)(2,1)S(1)}, u32[]{:S(2)}, u32[]{:S(2)}) %all-to-all-start.1) | async-done | bytes 1048608 | tf_op jit(solution)/shard_map/all_to_all | solution.py:275
  106.1 0.0 copy-start
  106.1 1.0 copy-done
  107.1 16.9 %drift.1 = f32[512,4,128]{2,1,0:T(4,128)} custom-call(s32[4]{0:T(128)} %select_reduce_fusion.low_ref, bf16[16,32,1024]{2,1,0:T(8,128)(2,1)} %copy-done), custom_call_target="tpu_custom_call" | custom-call | tf_op jit(solution)/shard_map/drift/pallas_call | solution.py:245
  124.0 2.6 %reshape.32 = f32[8,4,16,512]{3,2,1,0:T(8,128)} reshape(f32[512,4,128]{2,1,0:T(4,128)} %drift.1) | data formatting | bytes 2097152 | tf_op jit(solution)/shard_map/reshape | solution.py:278
  (3 shorter events, 0.0 us)
Async XLA Ops:
  1.0 7.8 %collective-permute-start = (bf16[8,4,8,512]{3,2,1,0:T(8,128)(2,1)S(1)}, bf16[8,4,8,512]{3,2,1,0:T(8,128)(2,1)S(1)}, u32[]{:S(2)}, u32[]{:S(2)}) collective-permute-start(bf16[8,4,8,512]{3,2,1,0:T(8,128)(2,1)S(1)} %slice.12), channel_id=1, source_target_pairs={{1,0},{2,1},{3,2},{4,3},{5,4},{6,5},{7,6},{8,7},{9,8},{10,9},{11,1... | collective-permute-start | bytes 786440 | tf_op jit(solution)/shard_map/ppermute | solution.py:269
  8.8 0.7 copy-start.1
  54.0 22.3 %copy-start.2 = (s32[512]{0:T(512)S(1)}, s32[512]{0:T(512)}, u32[]{:S(2)}) copy-start(s32[512]{0:T(512)} %param.11) | copy-start | bytes 6148
  54.0 22.9 %copy-start.3 = (s32[512]{0:T(512)S(1)}, s32[512]{0:T(512)}, u32[]{:S(2)}) copy-start(s32[512]{0:T(512)} %param.12) | copy-start | bytes 6148
  64.9 41.2 %all-to-all-start.1 = ((bf16[16,32,1024]{2,1,0:T(8,128)(2,1)}), bf16[16,32,1024]{2,1,0:T(8,128)(2,1)S(1)}, u32[]{:S(2)}, u32[]{:S(2)}) async-start(bf16[16,32,1024]{2,1,0:T(8,128)(2,1)} %bitcast.5), calls=%async_computation.1 | async-start | bytes 2097152 | tf_op jit(solution)/shard_map/all_to_all | solution.py:275
  106.1 1.0 copy-start

commit v2 on v0

v2 whole, which is shorter than its diff:
```python
import math

import jax
import jax.numpy as jnp
import numpy as np
from jax import lax
from jax.experimental import pallas as pl
from jax.experimental.pallas import tpu as pltpu
from jax.sharding import Mesh, PartitionSpec as P

TAPS = 4
NDRIFT = 16
N = 512
FINE = 2048
BEAMS = 8
STEPS = 16
BLK = 128
GRP = 16
WIN = 768
BINS = 512
BPS = 2
f32 = jnp.float32
bf16 = jnp.bfloat16


def np_bf16(a):
    return np.asarray(a, np.float32).astype(jnp.bfloat16)


def fine_tables():
    k = np.arange(GRP)
    ang = (k[:, None] * k[None, :]) % GRP * (2.0 * math.pi / GRP)
    c, sn = np.cos(ang), np.sin(ang)
    eye = np.eye(16)
    first = np.zeros((GRP, 2, 16, GRP, 2, 16))
    for q, p, val in ((0, 0, c), (0, 1, sn), (1, 0, -sn), (1, 1, c)):
        first[:, q, :, :, p, :] = val[:, None, :, None] * eye[None, :, None, :]
    f1 = np.arange(GRP)
    lane = np.arange(BLK)
    block = (lane[None, :] // 16 - f1[:, None]) % 8
    f2 = block * 16 + lane[None, :] % 16
    j = np.arange(BLK)
    ang = (j[None, :, None] * (f1[:, None] + 16 * f2)[:, None, :]) % FINE * (2.0 * math.pi / FINE)
    c, sn = np.cos(ang), np.sin(ang)
    second = np.concatenate([np.concatenate([c, -sn], 2), np.concatenate([sn, c], 2)], 1)
    perm = np.zeros((256, 256))
    for h in range(2):
        perm[h * 128 + lane, 8 * h + lane // 16 + 16 * (lane % 16)] = 1.0
    return np_bf16(first.reshape(512, 512)), np_bf16(second), np_bf16(perm)


def cos_sin(phase):
    quarter = lax.shift_right_arithmetic(phase + 64, 7)
    x = (phase - quarter * 128).astype(f32) * (2.0 * math.pi / N)
    y = x * x
    c = 1.0 + y * (-0.5 + y * (1.0 / 24 + y * (-1.0 / 720 + y * (1.0 / 40320))))
    s = x * (1.0 + y * (-1.0 / 6 + y * (1.0 / 120 + y * (-1.0 / 5040 + y * (1.0 / 362880)))))
    swap = (quarter & 1) == 1
    cos = jnp.where(swap, s, c)
    sin = jnp.where(swap, c, s)
    cos = jnp.where(((quarter + 1) & 2) == 2, -cos, cos)
    sin = jnp.where((quarter & 2) == 2, -sin, sin)
    return cos, sin


def write_tables(mask_ref, low_ref, wt_ref, rate_ref):
    row = lax.broadcasted_iota(jnp.int32, (N, N), 0)
    col = lax.broadcasted_iota(jnp.int32, (N, N), 1)
    upper = (row < col).astype(f32).astype(bf16)
    mask = jnp.broadcast_to(mask_ref[...], (8, N))
    before = jnp.dot(mask.astype(f32).astype(bf16), upper, preferred_element_type=f32)[0:1].astype(jnp.int32)
    before = jnp.where(mask_ref[...] == 1, before, -1)
    for r0 in range(0, 256, 16):
        rp = r0 + lax.broadcasted_iota(jnp.int32, (16, N), 0)
        pos = lax.broadcasted_iota(jnp.int32, (16, N), 1)
        hit = before == (rp // 4) % 4 * 64 + rp // 16 * 4 + rp % 4
        rate_ref[r0 : r0 + 16] = jnp.sum(jnp.where(hit, low_ref[...], 0), axis=1, keepdims=True)
        chan = jnp.sum(jnp.where(hit, pos, 0), axis=1, keepdims=True)
        cos, sin = cos_sin((chan * pos) & (N - 1))
        wt_ref[r0 // 16, 0:16, 0:N] = cos.astype(bf16)
        wt_ref[r0 // 16, 0:16, N : 2 * N] = sin.astype(bf16)
        wt_ref[r0 // 16, 16:32, 0:N] = (-sin).astype(bf16)
        wt_ref[r0 // 16, 16:32, N : 2 * N] = cos.astype(bf16)


def front_kernel(mask_ref, low_ref, taps_ref, v_ref, wt_ref, rate_ref, filt_ref, ext_ref):
    @pl.when(pl.program_id(0) == 0)
    def _():
        write_tables(mask_ref, low_ref, wt_ref, rate_ref)
        for c in range(N // 128):
            ext_ref[c, BLK : BLK + 8, :] = jnp.zeros((8, 128), f32)

    def body(bo, carry):
        b = bo // 4
        op = bo % 4
        row = pl.multiple_of((op // 2) * BLK, BLK)
        for c in range(N // 128):
            lanes = pl.ds(c * 128, 128)
            main = v_ref[b, op, :, lanes].astype(f32)
            ext_ref[c, 0:BLK, :] = main
            acc = taps_ref[0:1, lanes] * main
            for tap in range(1, TAPS):
                acc = acc + taps_ref[tap : tap + 1, lanes] * ext_ref[c, tap : tap + BLK, :]
            at = pl.multiple_of((op % 2) * N + c * 128, 128)
            filt_ref[b, pl.ds(row, BLK), pl.ds(at, 128)] = acc.astype(bf16)
        return carry

    lax.fori_loop(0, BPS * 4, body, 0)


def front(mask, low, taps, volt):
    whole = lambda shape: pl.BlockSpec(shape, lambda b: (0,) * len(shape))
    return pl.pallas_call(
        front_kernel,
        grid=(BEAMS // BPS,),
        in_specs=[
            whole((1, N)),
            whole((1, N)),
            whole((TAPS, N)),
            pl.BlockSpec((BPS, 4, BLK, N), lambda b: (b, 0, 0, 0)),
        ],
        out_specs=(
            whole((GRP, 32, 2 * N)),
            whole((256, 1)),
            pl.BlockSpec((BPS, 256, 2 * N), lambda b: (b, 0, 0)),
        ),
        out_shape=(
            jax.ShapeDtypeStruct((GRP, 32, 2 * N), bf16),
            jax.ShapeDtypeStruct((256, 1), jnp.int32),
            jax.ShapeDtypeStruct((BEAMS, 256, 2 * N), bf16),
        ),
        scratch_shapes=[pltpu.VMEM((N // 128, BLK + 8, 128), f32)],
        compiler_params=pltpu.CompilerParams(vmem_limit_bytes=57 << 20),
        name="front",
    )(mask, low, taps, volt)


def coarse_kernel(tail_ref, halo_ref, taps_ref, wt_ref, filt_ref, out_ref, buf_ref, ext_ref, res_ref, in_sem, out_sem):
    fetch = [pltpu.make_async_copy(filt_ref.at[b], buf_ref.at[b], in_sem.at[b]) for b in range(BEAMS)]
    send = [pltpu.make_async_copy(res_ref.at[b], out_ref.at[:, b], out_sem.at[b]) for b in range(BEAMS)]
    for copy in fetch:
        copy.start()
    for b in range(BEAMS):
        fetch[b].wait()
        for op in range(4):
            o, p = divmod(op, 2)
            for c in range(N // 128):
                lanes = pl.ds(c * 128, 128)
                slot = (b % 2) * 16 + op * 4 + c
                ext_ref[slot, 0:8, :] = tail_ref[b, op, :, lanes].astype(f32)
                ext_ref[slot, 8:16, :] = halo_ref[b, op, :, lanes].astype(f32)
                acc = taps_ref[0:1, lanes] * ext_ref[slot, 0:8, :]
                for tap in range(1, TAPS):
                    acc = acc + taps_ref[tap : tap + 1, lanes] * ext_ref[slot, tap : tap + 8, :]
                buf_ref[b, (o + 1) * BLK - 8 : (o + 1) * BLK, p * N + c * 128 : p * N + (c + 1) * 128] = acc.astype(bf16)
        for h in range(2):
            half = slice(h * GRP // 2, (h + 1) * GRP // 2)
            res = lax.dot_general(
                wt_ref[half].reshape(256, 2 * N),
                buf_ref[b],
                (((1,), (1,)), ((), ())),
                preferred_element_type=f32,
            )
            res_ref[b, half] = (res * (N ** -0.5)).astype(bf16).reshape(GRP // 2, 32, 256)
        send[b].start()
    for copy in send:
        copy.wait()


def coarse(volt, halo, taps, wt, filt):
    whole = lambda shape: pl.BlockSpec(shape, lambda b: (0,) * len(shape))
    return pl.pallas_call(
        coarse_kernel,
        grid=(1,),
        in_specs=[
            pl.BlockSpec((BEAMS, 4, 8, N), lambda b: (0, 0, BLK // 8 - 1, 0)),
            whole((BEAMS, 4, 8, N)),
            whole((TAPS, N)),
            whole((GRP, 32, 2 * N)),
            pl.BlockSpec(memory_space=pltpu.HBM),
        ],
        out_specs=pl.BlockSpec(memory_space=pltpu.HBM),
        out_shape=jax.ShapeDtypeStruct((GRP, BEAMS, 32, 256), bf16),
        scratch_shapes=[
            pltpu.VMEM((BEAMS, 256, 2 * N), bf16),
            pltpu.VMEM((32, 16, 128), f32),
            pltpu.VMEM((BEAMS, GRP, 32, 256), bf16),
            pltpu.SemaphoreType.DMA((BEAMS,)),
            pltpu.SemaphoreType.DMA((BEAMS,)),
        ],
        compiler_params=pltpu.CompilerParams(vmem_limit_bytes=56 << 20),
        name="coarse",
    )(volt, halo, taps, wt, filt)


def fine_kernel(rate_ref, x_ref, first_ref, second_hbm, perm_ref, out_ref, second_ref, lhs_ref, mix_ref, pow_ref, pow2_ref, sem):
    load = pltpu.make_async_copy(second_hbm, second_ref, sem)
    load.start()

    def beam(b, carry):
        rows = pl.ds(pl.multiple_of(b * 16, 16), 16)
        x = x_ref[:, b].reshape(512, 256)
        for h in range(2):
            y = jnp.dot(first_ref[h * 256 : (h + 1) * 256], x, preferred_element_type=f32).astype(bf16)
            for f in range(8):
                for q in range(2):
                    part = y[(2 * f + q) * 16 : (2 * f + q + 1) * 16]
                    for o in range(2):
                        lhs_ref[8 * h + f, o, rows, q * BLK : (q + 1) * BLK] = part[:, o * BLK : (o + 1) * BLK]
        return carry

    lax.fori_loop(0, BEAMS, beam, 0, unroll=2)
    load.wait()
    for f in range(GRP):
        total = None
        for o in range(2):
            z = jnp.dot(lhs_ref[f, o], second_ref[f], preferred_element_type=f32)
            part = z[:, 0:BLK] * z[:, 0:BLK] + z[:, BLK : 2 * BLK] * z[:, BLK : 2 * BLK]
            total = part if total is None else total + part
        pow2_ref[f] = total * (1.0 / 8192.0)
    lane = lax.broadcasted_iota(jnp.int32, (16, 128), 1)

    def mix(b, carry):
        rows = pl.ds(pl.multiple_of(b * 16, 16), 16)
        for h in range(2):
            v = [pow2_ref[8 * h + i, rows, :] for i in range(8)]
            for bit in (1, 2, 4):
                odd = (lane // (16 * bit)) % 2 == 1
                v = [jnp.where(odd, v[(m + bit) % 8], v[m]) for m in range(8)]
            for m in range(8):
                mix_ref[(8 - m) % 8, rows, h * 128 : (h + 1) * 128] = v[m].astype(bf16)
        return carry

    lax.fori_loop(0, BEAMS, mix, 0, unroll=2)
    zero = jnp.zeros((128, 128), f32)
    for e in (0, 1, 18, 19, 20):
        pow_ref[e] = zero
    for m in range(8):
        spots = [h * BLK + 16 * ((p - m) % 8) for h in range(2) for p in range(8)]
        turned = jnp.concatenate([perm_ref[r : r + 16] for r in spots], axis=0)
        q = jnp.dot(mix_ref[m], turned, preferred_element_type=f32)
        for h in range(2):
            for b in range(BEAMS):
                tile = q[b * 16 : (b + 1) * 16, h * 128 : (h + 1) * 128]
                pow_ref[2 + 2 * m + h, pl.ds(b, 16, stride=8), :] = tile
    low_lane = lax.broadcasted_iota(jnp.int32, (8, 128), 1)
    step = rate_ref[16]

    def shift(ch, carry):
        start = 256 + rate_ref[ch] * step
        base = lax.shift_right_logical(start, 7)
        off = start & 127
        rows = pl.ds(pl.multiple_of(ch * 8, 8), 8)
        last = low_lane >= off
        r = [pow_ref[base + k, rows, :] for k in range(19)]
        for k in range(18):
            pow2_ref[k, rows, :] = pltpu.roll(jnp.where(last, r[k], r[k + 1]), (128 - off) & 127, 1)
        return carry

    lax.fori_loop(0, 16, shift, 0, unroll=4)
    for x in range(4):
        for w in range(WIN // 128):
            out_ref[x, :, w * 128 : (w + 1) * 128] = pow2_ref[4 * x + w].astype(bf16)


def fine(rates, x, first, second, perm):
    vmem = pl.BlockSpec(memory_space=pltpu.VMEM)
    return pl.pallas_call(
        fine_kernel,
        in_specs=[
            pl.BlockSpec(memory_space=pltpu.SMEM),
            vmem,
            vmem,
            pl.BlockSpec(memory_space=pltpu.HBM),
            vmem,
        ],
        out_specs=vmem,
        out_shape=jax.ShapeDtypeStruct((4, 128, WIN), bf16),
        scratch_shapes=[
            pltpu.VMEM((GRP, 256, 256), bf16),
            pltpu.VMEM((GRP, 2, 128, 256), bf16),
            pltpu.VMEM((8, 128, 256), bf16),
            pltpu.VMEM((21, 128, 128), f32),
            pltpu.VMEM((18, 128, 128), f32),
            pltpu.SemaphoreType.DMA,
        ],
        compiler_params=pltpu.CompilerParams(vmem_limit_bytes=56 << 20),
        name="fine",
    )(rates, x, first, second, perm)


def drift_kernel(x_ref, out_ref, wide_ref, sum_ref):
    for t in range(STEPS):
        for w in range(WIN // 128):
            wide_ref[t, w] = x_ref[t, :, w * 128 : (w + 1) * 128].astype(f32)
    lane = lax.broadcasted_iota(jnp.int32, (8, 128), 1)

    def body(i, carry):
        rows = pl.ds(pl.multiple_of(i * 8, 8), 8)
        for j in range(NDRIFT):
            acc = None
            for t in range(STEPS):
                base, off = divmod(j * t, 128)
                if off == 0:
                    w = [wide_ref[t, base + k, rows, :] for k in range(4)]
                else:
                    r = [wide_ref[t, base + k, rows, :] for k in range(5)]
                    w = [pltpu.roll(jnp.where(lane >= off, r[k], r[k + 1]), 128 - off, 1) for k in range(4)]
                acc = w if acc is None else [acc[k] + w[k] for k in range(4)]
            for k in range(4):
                sum_ref[k, pl.ds(i * NDRIFT + j, 8, stride=64), :] = acc[k] * (1.0 / STEPS)
        return carry

    lax.fori_loop(0, 4, body, 0)
    for k in range(4):
        out_ref[:, k * 128 : (k + 1) * 128] = sum_ref[k]


def drift(x):
    return pl.pallas_call(
        drift_kernel,
        in_specs=[pl.BlockSpec(memory_space=pltpu.VMEM)],
        out_specs=pl.BlockSpec(memory_space=pltpu.VMEM),
        out_shape=jax.ShapeDtypeStruct((BEAMS * 64, BINS), f32),
        scratch_shapes=[
            pltpu.VMEM((STEPS, WIN // 128, 32, 128), f32),
            pltpu.VMEM((4, BEAMS * 64, 128), f32),
        ],
        compiler_params=pltpu.CompilerParams(vmem_limit_bytes=56 << 20),
        name="drift",
    )(x)


def shards(voltages, taps, busy_mask, drift_low):
    axes = ("x", "zh", "zl", "y", "core")
    devices = lax.axis_size(axes)
    head = lax.slice_in_dim(voltages, 0, 8, axis=2)
    halo = lax.ppermute(head, axes, [(i + 1, i) for i in range(devices - 1)])
    first, second, perm = fine_tables()
    wt, rates, filt = front(
        busy_mask.reshape(1, N), drift_low.reshape(1, N), taps, voltages
    )
    blocks = coarse(voltages, halo, taps, wt, filt)
    mine = lax.dynamic_slice_in_dim(rates.reshape(256), lax.axis_index(("zl", "y", "core")) * 16, 16)
    step = lax.axis_index(("x", "zh")).astype(jnp.int32).reshape(1)
    rate, blocks = lax.optimization_barrier((jnp.concatenate([mine, step]), blocks))
    times = lax.all_to_all(blocks, ("zl", "y", "core"), split_axis=0, concat_axis=0, tiled=True)
    powers = fine(rate, times, jnp.asarray(first), jnp.asarray(second), jnp.asarray(perm))
    wins = lax.all_to_all(powers.reshape(16, 32, WIN), ("x", "zh"), split_axis=0, concat_axis=0, tiled=True)
    out = drift(wins)
    return out.reshape(BEAMS, 4, NDRIFT, BINS)


def solution(mesh):
    fold = Mesh(mesh.devices.reshape(4, 4, 2, 4, 2), ("x", "zh", "zl", "y", "core"))
    chan = ("zh", "zl", "y", "core")
    in_specs = (P(None, None, ("x",) + chan, None), P(), P(), P())
    out_specs = P(None, chan, None, "x")
    return jax.shard_map(shards, mesh=fold, in_specs=in_specs, out_specs=out_specs, check_vma=False)
```

time: 277 us -> 103 us (0.37)
  between operations: 166 us -> 0.05 us
  blocking collectives: 30.9 us -> 66.3 us
  local copies, waits for them, and re-layouts: 37.3 us -> 2.5 us
  Pallas kernels: 0 us -> 29 us
  other arithmetic: 18.4 us -> 0.65 us
  starting transfers between devices: 13.8 us -> 3.91 us
  matrix products: 8.46 us -> 0 us
    all_to_all x1 -> x2, blocking collectives: 30.9 us -> 66.3 us  [the longest x1 35.8 us: shards(): lax.all_to_all(powers.reshape(16, 32, WIN), ('x', 'zh'), split_axis=0, co...]
    pallas_call x0 -> x4, Pallas kernels: none -> 29 us  [the longest x1 8.3 us: front(): pl.pallas_call(front_kernel, grid=(BEAMS // BPS,), in_specs=[whole((1, N)...]
    convert_element_type x1 -> x0, other arithmetic: 10.8 us -> none  [shards(): filtered.astype(jnp.bfloat16)]
    all_to_all x1 -> x0, starting transfers between devices: 9.89 us -> none  [shards(): lax.all_to_all(coarse, 'chan', split_axis=2, concat_axis=3, tiled=True)]
    dot_general x3 -> x0, matrix products: 8.46 us -> none  [the longest x1 3.48 us: detect_power(): jnp.einsum('xopctab,paqf->xoqctfb', shaped, real_dft(short_ids, short_ids...]
    div x3 -> x0, local copies, waits for them, and re-layouts: 8.19 us -> none  [the longest x2 6.61 us: detect_power(): powers = jnp.sum(second_pass * second_pass, axis=(1, 2)) / (4.0 * FA * FB)]
    unnamed x249 -> x2, local copies, waits for them, and re-layouts: 7.68 us -> 0.72 us
    reshape x2 -> x0, local copies, waits for them, and re-layouts: 6.25 us -> none  [the longest x1 3.3 us: detect_power(): shaped = spectra.reshape(items, 2, 2, chan_rows, step_count, FA, FB)]
  transfers between devices with their start and end apart: 2 -> 1, of which waited for: 0 -> 0; matrix products, arithmetic and copies ran while one was open for 4% -> 1% of each run, Pallas kernels for 0% -> 8%
where the time goes in v2:
time: 103 us; the launch traced here: 102 us
  blocking collectives  66.3 us (64%)
  Pallas kernels  29 us (28%)
  starting transfers between devices  3.91 us (4%)
  local copies, waits for them, and re-layouts  2.5 us (2%)
    all_to_all x1, blocking collectives, shards(): lax.all_to_all(powers.reshape(16, 32, WIN), ('x', 'zh'), split_axis=0, co...  35.8 us
    all_to_all x1, blocking collectives, shards(): lax.all_to_all(blocks, ('zl', 'y', 'core'), split_axis=0, concat_axis=0,...  30.5 us
    pallas_call x1, Pallas kernels, front(): pl.pallas_call(front_kernel, grid=(BEAMS // BPS,), in_specs=[whole((1, N)...  8.3 us
    pallas_call x1, Pallas kernels, coarse(): pl.pallas_call(coarse_kernel, grid=(1,), in_specs=[pl.BlockSpec((BEAMS, 4...  7.27 us
    pallas_call x1, Pallas kernels, drift(): pl.pallas_call(drift_kernel, in_specs=[pl.BlockSpec(memory_space=pltpu.VM...  6.95 us
    pallas_call x1, Pallas kernels, fine(): pl.pallas_call(fine_kernel, in_specs=[pl.BlockSpec(memory_space=pltpu.SME...  6.45 us
    ppermute x1, starting transfers between devices, shards(): halo = lax.ppermute(head, axes, [(i + 1, i) for i in range(devices - 1)])  3.91 us
  transfers between devices with their start and end apart: 1, of which 0 were waited for; matrix products, arithmetic and copies ran while one was open for 1% of the time, Pallas kernels for 8%

profile of v2, /device:TPU:32, one launch (start us, length us, event | category | flops | bytes accessed | tf_op | source)
XLA Modules:
  0.0 102.3 jit_solution(1773675247753785559)
XLA Ops:
  0.0 1.0 slice.3
  1.0 3.9 %collective-permute-start = (bf16[8,4,8,512]{3,2,1,0:T(8,128)(2,1)S(1)}, bf16[8,4,8,512]{3,2,1,0:T(8,128)(2,1)S(1)}, u32[]{:S(2)}, u32[]{:S(2)}) collective-permute-start(bf16[8,4,8,512]{3,2,1,0:T(8,128)(2,1)S(1)} %slice.3), channel_id=1, source_target_pairs={{1,0},{2,1},{3,2},{4,3},{5,4},{6,5},{7,6},{8,7},{9,8},{10,9},{11,1... | collective-permute-start | bytes 786440 | tf_op jit(solution)/shard_map/ppermute | solution.py:338
  4.9 8.3 %front.1 = (bf16[16,32,1024]{2,1,0:T(8,128)(2,1)}, s32[256,1]{1,0:T(8,128)}, bf16[8,256,1024]{2,1,0:T(8,128)(2,1)}) custom-call(s32[1,512]{1,0:T(1,128)} %bitcast.6, s32[1,512]{1,0:T(1,128)} %bitcast.7, f32[4,512]{1,0:T(4,128)} %taps_ref.3, bf16[8,4,128,512]{3,2,1,0:T(8,128)(2,1)} %tail_ref.1), custom_call_target="tpu_custom_call" | custom-call | tf_op jit(solution)/shard_map/front/pallas_call | solution.py:113
  13.2 0.8 dynamic-slice_reduce_fusion
  14.0 0.7 pad_add_fusion.rate_ref
  14.7 0.0 collective-permute-done.halo_ref
  14.7 0.0 copy-start
  14.7 0.7 copy-done
  15.4 7.3 %coarse.1 = bf16[16,8,32,256]{3,2,1,0:T(8,128)(2,1)} custom-call(bf16[8,4,128,512]{3,2,1,0:T(8,128)(2,1)} %tail_ref.1, bf16[8,4,8,512]{3,2,1,0:T(8,128)(2,1)} %copy-done, f32[4,512]{1,0:T(4,128)} %taps_ref.3, bf16[16,32,1024]{2,1,0:T(8,128)(2,1)} %get-tuple-element.11.wt_ref, bf16[8,256,1024]{2,1,0:T(8,128)(2,1)} %get-tuple-element.12.filt_ref), custom_call_target="tpu_custom_call" | custom-call | tf_op jit(solution)/shard_map/coarse/pallas_call | solution.py:172
  22.7 30.5 %all_to_all.10.x_ref = bf16[16,8,32,256]{3,2,1,0:T(8,128)(2,1)} all-to-all(bf16[16,8,32,256]{3,2,1,0:T(8,128)(2,1)} %coarse.1), channel_id=1, replica_groups=mesh['x'=4,'zh'=4,'zl'=2,'y'=4,'core'=2] {'zl','y','core'}, dimensions={0} | all-to-all | bytes 4194304 | tf_op jit(solution)/shard_map/all_to_all | solution.py:347
  53.2 6.5 %fine.1 = bf16[4,128,768]{2,1,0:T(8,128)(2,1)} custom-call(s32[17]{0:T(128)} %pad_add_fusion.rate_ref, bf16[16,8,32,256]{3,2,1,0:T(8,128)(2,1)} %all_to_all.10.x_ref, bf16[512,512]{1,0:T(8,128)(2,1)} %constant.38.clone.first_ref, bf16[16,256,256]{2,1,0:T(8,128)(2,1)} %constant.39.clone.second_hbm, bf16[256,256]{1,0:T(8,128)(2,1)} %constant.40.clone.perm_ref), custom_call_target="tpu_custom_call" | custom-call | tf_op jit(solution)/shard_map/fine/pallas_call | solution.py:268
  59.6 35.8 %all_to_all.11.x_ref = bf16[16,32,768]{2,1,0:T(8,128)(2,1)} all-to-all(bf16[16,32,768]{2,1,0:T(8,128)(2,1)} %bitcast.5), channel_id=1, replica_groups=mesh['x'=4,'zh'=4,'zl'=2,'y'=4,'core'=2] {'x','zh'}, dimensions={0} | all-to-all | bytes 1572864 | tf_op jit(solution)/shard_map/all_to_all | solution.py:349
  95.4 7.0 %drift.1 = f32[512,512]{1,0:T(8,128)} custom-call(bf16[16,32,768]{2,1,0:T(8,128)(2,1)} %all_to_all.11.x_ref), custom_call_target="tpu_custom_call" | custom-call | tf_op jit(solution)/shard_map/drift/pallas_call | solution.py:320
Async XLA Ops:
  1.0 13.7 %collective-permute-start = (bf16[8,4,8,512]{3,2,1,0:T(8,128)(2,1)S(1)}, bf16[8,4,8,512]{3,2,1,0:T(8,128)(2,1)S(1)}, u32[]{:S(2)}, u32[]{:S(2)}) collective-permute-start(bf16[8,4,8,512]{3,2,1,0:T(8,128)(2,1)S(1)} %slice.3), channel_id=1, source_target_pairs={{1,0},{2,1},{3,2},{4,3},{5,4},{6,5},{7,6},{8,7},{9,8},{10,9},{11,1... | collective-permute-start | bytes 786440 | tf_op jit(solution)/shard_map/ppermute | solution.py:338
  14.7 0.7 copy-start

commit v3 on v2

--- a/solution.py
+++ b/solution.py
@@ -63,32 +63,38 @@
     return cos, sin
 
 
-def write_tables(mask_ref, low_ref, wt_ref, rate_ref):
+def write_tables(small_ref, wt_ref, rate_ref, hit_ref):
+    busy = small_ref[TAPS : TAPS + 1]
     row = lax.broadcasted_iota(jnp.int32, (N, N), 0)
     col = lax.broadcasted_iota(jnp.int32, (N, N), 1)
     upper = (row < col).astype(f32).astype(bf16)
-    mask = jnp.broadcast_to(mask_ref[...], (8, N))
-    before = jnp.dot(mask.astype(f32).astype(bf16), upper, preferred_element_type=f32)[0:1].astype(jnp.int32)
-    before = jnp.where(mask_ref[...] == 1, before, -1)
+    mask = jnp.broadcast_to(busy, (8, N))
+    before = jnp.dot(mask.astype(bf16), upper, preferred_element_type=f32)[0:1].astype(jnp.int32)
+    before = jnp.where(busy > 0.5, before, -1)
     for r0 in range(0, 256, 16):
         rp = r0 + lax.broadcasted_iota(jnp.int32, (16, N), 0)
         pos = lax.broadcasted_iota(jnp.int32, (16, N), 1)
         hit = before == (rp // 4) % 4 * 64 + rp // 16 * 4 + rp % 4
-        rate_ref[r0 : r0 + 16] = jnp.sum(jnp.where(hit, low_ref[...], 0), axis=1, keepdims=True)
+        hit_ref[r0 : r0 + 16] = hit.astype(f32).astype(bf16)
         chan = jnp.sum(jnp.where(hit, pos, 0), axis=1, keepdims=True)
         cos, sin = cos_sin((chan * pos) & (N - 1))
         wt_ref[r0 // 16, 0:16, 0:N] = cos.astype(bf16)
         wt_ref[r0 // 16, 0:16, N : 2 * N] = sin.astype(bf16)
         wt_ref[r0 // 16, 16:32, 0:N] = (-sin).astype(bf16)
         wt_ref[r0 // 16, 16:32, N : 2 * N] = cos.astype(bf16)
-
-
-def front_kernel(mask_ref, low_ref, taps_ref, v_ref, wt_ref, rate_ref, filt_ref, ext_ref):
+    low = jnp.broadcast_to(small_ref[TAPS + 1 : TAPS + 2], (8, N)).astype(bf16)
+    rate = lax.dot_general(low, hit_ref[...], (((1,), (1,)), ((), ())), preferred_element_type=f32)
+    rate_ref[...] = rate[0:1].astype(jnp.int32)
+
+
+def front_kernel(small_ref, v_ref, wt_ref, rate_ref, tail_ref, filt_ref, ext_ref, hit_ref):
     @pl.when(pl.program_id(0) == 0)
     def _():
-        write_tables(mask_ref, low_ref, wt_ref, rate_ref)
+        write_tables(small_ref, wt_ref, rate_ref, hit_ref)
         for c in range(N // 128):
             ext_ref[c, BLK : BLK + 8, :] = jnp.zeros((8, 128), f32)
+
+    tail_ref[...] = v_ref[:, :, BLK - 8 : BLK, :]
 
     def body(bo, carry):
         b = bo // 4
@@ -98,9 +104,9 @@
             lanes = pl.ds(c * 128, 128)
             main = v_ref[b, op, :, lanes].astype(f32)
             ext_ref[c, 0:BLK, :] = main
-            acc = taps_ref[0:1, lanes] * main
+            acc = small_ref[0:1, lanes] * main
             for tap in range(1, TAPS):
-                acc = acc + taps_ref[tap : tap + 1, lanes] * ext_ref[c, tap : tap + BLK, :]
+                acc = acc + small_ref[tap : tap + 1, lanes] * ext_ref[c, tap : tap + BLK, :]
             at = pl.multiple_of((op % 2) * N + c * 128, 128)
             filt_ref[b, pl.ds(row, BLK), pl.ds(at, 128)] = acc.astype(bf16)
         return carry
@@ -108,31 +114,28 @@
     lax.fori_loop(0, BPS * 4, body, 0)
 
 
-def front(mask, low, taps, volt):
+def front(small, volt):
     whole = lambda shape: pl.BlockSpec(shape, lambda b: (0,) * len(shape))
     return pl.pallas_call(
         front_kernel,
         grid=(BEAMS // BPS,),
-        in_specs=[
-            whole((1, N)),
-            whole((1, N)),
-            whole((TAPS, N)),
-            pl.BlockSpec((BPS, 4, BLK, N), lambda b: (b, 0, 0, 0)),
-        ],
+        in_specs=[whole((8, N)), pl.BlockSpec((BPS, 4, BLK, N), lambda b: (b, 0, 0, 0))],
         out_specs=(
             whole((GRP, 32, 2 * N)),
-            whole((256, 1)),
+            whole((1, 256)),
+            pl.BlockSpec((BPS, 4, 8, N), lambda b: (b, 0, 0, 0)),
             pl.BlockSpec((BPS, 256, 2 * N), lambda b: (b, 0, 0)),
         ),
         out_shape=(
             jax.ShapeDtypeStruct((GRP, 32, 2 * N), bf16),
-            jax.ShapeDtypeStruct((256, 1), jnp.int32),
+            jax.ShapeDtypeStruct((1, 256), jnp.int32),
+            jax.ShapeDtypeStruct((BEAMS, 4, 8, N), bf16),
             jax.ShapeDtypeStruct((BEAMS, 256, 2 * N), bf16),
         ),
-        scratch_shapes=[pltpu.VMEM((N // 128, BLK + 8, 128), f32)],
-        compiler_params=pltpu.CompilerParams(vmem_limit_bytes=57 << 20),
+        scratch_shapes=[pltpu.VMEM((N // 128, BLK + 8, 128), f32), pltpu.VMEM((256, N), bf16)],
+        compiler_params=pltpu.CompilerParams(vmem_limit_bytes=46 << 20),
         name="front",
-    )(mask, low, taps, volt)
+    )(small, volt)
 
 
 def coarse_kernel(tail_ref, halo_ref, taps_ref, wt_ref, filt_ref, out_ref, buf_ref, ext_ref, res_ref, in_sem, out_sem):
@@ -167,15 +170,15 @@
         copy.wait()
 
 
-def coarse(volt, halo, taps, wt, filt):
+def coarse(tail, halo, small, wt, filt):
     whole = lambda shape: pl.BlockSpec(shape, lambda b: (0,) * len(shape))
     return pl.pallas_call(
         coarse_kernel,
         grid=(1,),
         in_specs=[
-            pl.BlockSpec((BEAMS, 4, 8, N), lambda b: (0, 0, BLK // 8 - 1, 0)),
             whole((BEAMS, 4, 8, N)),
-            whole((TAPS, N)),
+            whole((BEAMS, 4, 8, N)),
+            whole((8, N)),
             whole((GRP, 32, 2 * N)),
             pl.BlockSpec(memory_space=pltpu.HBM),
         ],
@@ -188,9 +191,9 @@
             pltpu.SemaphoreType.DMA((BEAMS,)),
             pltpu.SemaphoreType.DMA((BEAMS,)),
         ],
-        compiler_params=pltpu.CompilerParams(vmem_limit_bytes=56 << 20),
+        compiler_params=pltpu.CompilerParams(vmem_limit_bytes=46 << 20),
         name="coarse",
-    )(volt, halo, taps, wt, filt)
+    )(tail, halo, small, wt, filt)
 
 
 def fine_kernel(rate_ref, x_ref, first_ref, second_hbm, perm_ref, out_ref, second_ref, lhs_ref, mix_ref, pow_ref, pow2_ref, sem):
@@ -244,10 +247,11 @@
                 tile = q[b * 16 : (b + 1) * 16, h * 128 : (h + 1) * 128]
                 pow_ref[2 + 2 * m + h, pl.ds(b, 16, stride=8), :] = tile
     low_lane = lax.broadcasted_iota(jnp.int32, (8, 128), 1)
-    step = rate_ref[16]
+    step = lax.axis_index(("x", "zh"))
+    own = lax.axis_index(("zl", "y", "core")) * 16
 
     def shift(ch, carry):
-        start = 256 + rate_ref[ch] * step
+        start = 256 + rate_ref[0, own + ch] * step
         base = lax.shift_right_logical(start, 7)
         off = start & 127
         rows = pl.ds(pl.multiple_of(ch * 8, 8), 8)
@@ -284,7 +288,7 @@
             pltpu.VMEM((18, 128, 128), f32),
             pltpu.SemaphoreType.DMA,
         ],
-        compiler_params=pltpu.CompilerParams(vmem_limit_bytes=56 << 20),
+        compiler_params=pltpu.CompilerParams(vmem_limit_bytes=50 << 20),
         name="fine",
     )(rates, x, first, second, perm)
 
@@ -326,7 +330,7 @@
             pltpu.VMEM((STEPS, WIN // 128, 32, 128), f32),
             pltpu.VMEM((4, BEAMS * 64, 128), f32),
         ],
-        compiler_params=pltpu.CompilerParams(vmem_limit_bytes=56 << 20),
+        compiler_params=pltpu.CompilerParams(vmem_limit_bytes=50 << 20),
         name="drift",
     )(x)
 
@@ -337,15 +341,12 @@
     head = lax.slice_in_dim(voltages, 0, 8, axis=2)
     halo = lax.ppermute(head, axes, [(i + 1, i) for i in range(devices - 1)])
     first, second, perm = fine_tables()
-    wt, rates, filt = front(
-        busy_mask.reshape(1, N), drift_low.reshape(1, N), taps, voltages
-    )
-    blocks = coarse(voltages, halo, taps, wt, filt)
-    mine = lax.dynamic_slice_in_dim(rates.reshape(256), lax.axis_index(("zl", "y", "core")) * 16, 16)
-    step = lax.axis_index(("x", "zh")).astype(jnp.int32).reshape(1)
-    rate, blocks = lax.optimization_barrier((jnp.concatenate([mine, step]), blocks))
+    extra = jnp.stack([busy_mask, drift_low]).astype(f32)
+    small = jnp.concatenate([taps, extra, jnp.zeros((2, N), f32)], axis=0)
+    wt, rates, tail, filt = front(small, voltages)
+    blocks = coarse(tail, halo, small, wt, filt)
     times = lax.all_to_all(blocks, ("zl", "y", "core"), split_axis=0, concat_axis=0, tiled=True)
-    powers = fine(rate, times, jnp.asarray(first), jnp.asarray(second), jnp.asarray(perm))
+    powers = fine(rates, times, jnp.asarray(first), jnp.asarray(second), jnp.asarray(perm))
     wins = lax.all_to_all(powers.reshape(16, 32, WIN), ("x", "zh"), split_axis=0, concat_axis=0, tiled=True)
     out = drift(wins)
     return out.reshape(BEAMS, 4, NDRIFT, BINS)

time: 103 us -> 92.7 us (0.900)
  Pallas kernels: 29 us -> 21.1 us
  blocking collectives: 66.3 us -> 64.7 us
  local copies, waits for them, and re-layouts: 2.5 us -> 1.06 us
    pallas_call x2, Pallas kernels: 15.6 us -> 11 us  [the longest x1 6.41 us: front(): pl.pallas_call(front_kernel, grid=(BEAMS // BPS,), in_specs=[whole((8, N)...]
    pallas_call x1, Pallas kernels: 6.45 us -> 4.35 us  [fine(): pl.pallas_call(fine_kernel, in_specs=[pl.BlockSpec(memory_space=pltpu.SME...]
    all_to_all x1, blocking collectives: 35.8 us -> 34.5 us  [shards(): lax.all_to_all(powers.reshape(16, 32, WIN), ('x', 'zh'), split_axis=0, co...]
    pallas_call x1, Pallas kernels: 6.95 us -> 5.82 us  [drift(): pl.pallas_call(drift_kernel, in_specs=[pl.BlockSpec(memory_space=pltpu.VM...]
  transfers between devices with their start and end apart: 1 -> 1, of which waited for: 0 -> 0; matrix products, arithmetic and copies ran while one was open for 1% -> 2% of each run, Pallas kernels for 8% -> 7%
where the time goes in v3:
time: 92.7 us; the launch traced here: 92.4 us
  blocking collectives  64.7 us (70%)
  Pallas kernels  21.1 us (23%)
  starting transfers between devices  3.91 us (4%)
  other arithmetic  1.48 us (2%)
  local copies, waits for them, and re-layouts  1.06 us (1%)
    all_to_all x1, blocking collectives, shards(): lax.all_to_all(powers.reshape(16, 32, WIN), ('x', 'zh'), split_axis=0, co...  34.5 us
    all_to_all x1, blocking collectives, shards(): lax.all_to_all(blocks, ('zl', 'y', 'core'), split_axis=0, concat_axis=0,...  30.2 us
    pallas_call x1, Pallas kernels, front(): pl.pallas_call(front_kernel, grid=(BEAMS // BPS,), in_specs=[whole((8, N)...  6.41 us
    pallas_call x1, Pallas kernels, drift(): pl.pallas_call(drift_kernel, in_specs=[pl.BlockSpec(memory_space=pltpu.VM...  5.82 us
    pallas_call x1, Pallas kernels, coarse(): pl.pallas_call(coarse_kernel, grid=(1,), in_specs=[whole((BEAMS, 4, 8, N)...  4.57 us
    pallas_call x1, Pallas kernels, fine(): pl.pallas_call(fine_kernel, in_specs=[pl.BlockSpec(memory_space=pltpu.SME...  4.35 us
    ppermute x1, starting transfers between devices, shards(): halo = lax.ppermute(head, axes, [(i + 1, i) for i in range(devices - 1)])  3.91 us
  transfers between devices with their start and end apart: 1, of which 0 were waited for; matrix products, arithmetic and copies ran while one was open for 2% of the time, Pallas kernels for 7%

profile of v3, /device:TPU:32, one launch (start us, length us, event | category | flops | bytes accessed | tf_op | source)
XLA Modules:
  0.0 92.4 jit_solution(4695143593265095903)
XLA Ops:
  0.0 1.0 %slice.3 = bf16[8,4,8,512]{3,2,1,0:T(8,128)(2,1)S(1)} slice(bf16[8,4,128,512]{3,2,1,0:T(8,128)(2,1)} %v_ref.1), slice={[0:8], [0:4], [0:8], [0:512]} | slice | bytes 524288 | tf_op jit(solution)/shard_map/slice | solution.py:341
  1.0 3.9 %collective-permute-start = (bf16[8,4,8,512]{3,2,1,0:T(8,128)(2,1)S(1)}, bf16[8,4,8,512]{3,2,1,0:T(8,128)(2,1)S(1)}, u32[]{:S(2)}, u32[]{:S(2)}) collective-permute-start(bf16[8,4,8,512]{3,2,1,0:T(8,128)(2,1)S(1)} %slice.3), channel_id=1, source_target_pairs={{1,0},{2,1},{3,2},{4,3},{5,4},{6,5},{7,6},{8,7},{9,8},{10,9},{11,1... | collective-permute-start | bytes 786440 | tf_op jit(solution)/shard_map/ppermute | solution.py:342
  4.9 0.7 add_convert_fusion
  5.6 0.1 pad.2.clone
  5.7 0.8 maximum_maximum_fusion.small_ref.taps_ref
  6.4 6.4 %front.1 = (bf16[16,32,1024]{2,1,0:T(8,128)(2,1)S(1)}, s32[1,256]{1,0:T(1,128)S(1)}, bf16[8,4,8,512]{3,2,1,0:T(8,128)(2,1)S(1)}, bf16[8,256,1024]{2,1,0:T(8,128)(2,1)S(1)}) custom-call(f32[8,512]{1,0:T(8,128)S(1)} %maximum_maximum_fusion.small_ref.taps_ref, bf16[8,4,128,512]{3,2,1,0:T(8,128)(2,1)} %v_ref.1), custom_call_target="tpu_custom_call" | custom-call | tf_op jit(solution)/shard_map/front/pallas_call | solution.py:119
  12.9 0.0 collective-permute-done.halo_ref
  12.9 4.6 %coarse.1 = bf16[16,8,32,256]{3,2,1,0:T(8,128)(2,1)S(1)} custom-call(bf16[8,4,8,512]{3,2,1,0:T(8,128)(2,1)S(1)} %get-tuple-element.10.tail_ref, bf16[8,4,8,512]{3,2,1,0:T(8,128)(2,1)S(1)} %collective-permute-done.halo_ref, f32[8,512]{1,0:T(8,128)S(1)} %maximum_maximum_fusion.small_ref.taps_ref, bf16[16,32,1024]{2,1,0:T(8,128)(2,1)S(1)} %get-tuple-element.11.wt_ref, ...), custom_call_target="tpu_custom_call" | custom-call | tf_op jit(solution)/shard_map/coarse/pallas_call | solution.py:175
  17.5 0.0 copy-start
  17.5 0.0 copy-start.1
  17.5 30.2 %all_to_all.10.x_ref = bf16[16,8,32,256]{3,2,1,0:T(8,128)(2,1)S(1)} all-to-all(bf16[16,8,32,256]{3,2,1,0:T(8,128)(2,1)S(1)} %coarse.1), channel_id=1, replica_groups=mesh['x'=4,'zh'=4,'zl'=2,'y'=4,'core'=2] {'zl','y','core'}, dimensions={0} | all-to-all | bytes 4194304 | tf_op jit(solution)/shard_map/all_to_all | solution.py:348
  47.7 0.0 copy-done
  47.7 0.0 copy-done.1
  47.7 4.3 %fine.1 = bf16[4,128,768]{2,1,0:T(8,128)(2,1)S(1)} custom-call(s32[1,256]{1,0:T(1,128)S(1)} %get-tuple-element.9.rate_ref, bf16[16,8,32,256]{3,2,1,0:T(8,128)(2,1)S(1)} %all_to_all.10.x_ref, bf16[512,512]{1,0:T(8,128)(2,1)S(1)} %copy-done, bf16[16,256,256]{2,1,0:T(8,128)(2,1)} %constant.9.clone.second_hbm, bf16[256,256]{1,0:T(8,128)(2,1)S(1)} %copy-done.1), custom_call_target="tpu_custom_call" | custom-call | tf_op jit(solution)/shard_map/fine/pallas_call | solution.py:272
  52.1 34.5 %all_to_all.11.x_ref = bf16[16,32,768]{2,1,0:T(8,128)(2,1)S(1)} all-to-all(bf16[16,32,768]{2,1,0:T(8,128)(2,1)S(1)} %bitcast.4), channel_id=1, replica_groups=mesh['x'=4,'zh'=4,'zl'=2,'y'=4,'core'=2] {'x','zh'}, dimensions={0} | all-to-all | bytes 1572864 | tf_op jit(solution)/shard_map/all_to_all | solution.py:350
  86.6 5.8 %drift.1 = f32[512,512]{1,0:T(8,128)} custom-call(bf16[16,32,768]{2,1,0:T(8,128)(2,1)S(1)} %all_to_all.11.x_ref), custom_call_target="tpu_custom_call" | custom-call | tf_op jit(solution)/shard_map/drift/pallas_call | solution.py:324
  (1 shorter events, 0.0 us)
Async XLA Ops:
  1.0 11.9 %collective-permute-start = (bf16[8,4,8,512]{3,2,1,0:T(8,128)(2,1)S(1)}, bf16[8,4,8,512]{3,2,1,0:T(8,128)(2,1)S(1)}, u32[]{:S(2)}, u32[]{:S(2)}) collective-permute-start(bf16[8,4,8,512]{3,2,1,0:T(8,128)(2,1)S(1)} %slice.3), channel_id=1, source_target_pairs={{1,0},{2,1},{3,2},{4,3},{5,4},{6,5},{7,6},{8,7},{9,8},{10,9},{11,1... | collective-permute-start | bytes 786440 | tf_op jit(solution)/shard_map/ppermute | solution.py:342
  17.5 30.2 %copy-start = (bf16[512,512]{1,0:T(8,128)(2,1)S(1)}, bf16[512,512]{1,0:T(8,128)(2,1)}, u32[]{:S(2)}) copy-start(bf16[512,512]{1,0:T(8,128)(2,1)} %constant.8.clone.first_ref) | copy-start | bytes 1572868
  17.5 30.2 %copy-start.1 = (bf16[256,256]{1,0:T(8,128)(2,1)S(1)}, bf16[256,256]{1,0:T(8,128)(2,1)}, u32[]{:S(2)}) copy-start(bf16[256,256]{1,0:T(8,128)(2,1)} %constant.10.clone.perm_ref) | copy-start | bytes 393220

commit v4 on v3

--- a/solution.py
+++ b/solution.py
@@ -77,11 +77,20 @@
         hit = before == (rp // 4) % 4 * 64 + rp // 16 * 4 + rp % 4
         hit_ref[r0 : r0 + 16] = hit.astype(f32).astype(bf16)
         chan = jnp.sum(jnp.where(hit, pos, 0), axis=1, keepdims=True)
-        cos, sin = cos_sin((chan * pos) & (N - 1))
-        wt_ref[r0 // 16, 0:16, 0:N] = cos.astype(bf16)
-        wt_ref[r0 // 16, 0:16, N : 2 * N] = sin.astype(bf16)
-        wt_ref[r0 // 16, 16:32, 0:N] = (-sin).astype(bf16)
-        wt_ref[r0 // 16, 16:32, N : 2 * N] = cos.astype(bf16)
+        cos, sin = cos_sin((chan * pos[:, 0:BLK]) & (N - 1))
+        for c in range(N // BLK):
+            turns = (chan * c) & 3
+            odd = (turns & 1) == 1
+            cos_sign = jnp.where((turns == 1) | (turns == 2), -1.0, 1.0)
+            sin_sign = jnp.where(turns >= 2, -1.0, 1.0)
+            cc = jnp.where(odd, sin, cos) * cos_sign
+            ss = jnp.where(odd, cos, sin) * sin_sign
+            lanes = slice(c * BLK, (c + 1) * BLK)
+            high = slice(N + c * BLK, N + (c + 1) * BLK)
+            wt_ref[r0 // 16, 0:16, lanes] = cc.astype(bf16)
+            wt_ref[r0 // 16, 0:16, high] = ss.astype(bf16)
+            wt_ref[r0 // 16, 16:32, lanes] = (-ss).astype(bf16)
+            wt_ref[r0 // 16, 16:32, high] = cc.astype(bf16)
     low = jnp.broadcast_to(small_ref[TAPS + 1 : TAPS + 2], (8, N)).astype(bf16)
     rate = lax.dot_general(low, hit_ref[...], (((1,), (1,)), ((), ())), preferred_element_type=f32)
     rate_ref[...] = rate[0:1].astype(jnp.int32)
@@ -111,7 +120,7 @@
             filt_ref[b, pl.ds(row, BLK), pl.ds(at, 128)] = acc.astype(bf16)
         return carry
 
-    lax.fori_loop(0, BPS * 4, body, 0)
+    lax.fori_loop(0, BPS * 4, body, 0, unroll=2)
 
 
 def front(small, volt):
@@ -212,7 +221,7 @@
                         lhs_ref[8 * h + f, o, rows, q * BLK : (q + 1) * BLK] = part[:, o * BLK : (o + 1) * BLK]
         return carry
 
-    lax.fori_loop(0, BEAMS, beam, 0, unroll=2)
+    lax.fori_loop(0, BEAMS, beam, 0, unroll=4)
     load.wait()
     for f in range(GRP):
         total = None
@@ -250,21 +259,25 @@
     step = lax.axis_index(("x", "zh"))
     own = lax.axis_index(("zl", "y", "core")) * 16
 
-    def shift(ch, carry):
-        start = 256 + rate_ref[0, own + ch] * step
-        base = lax.shift_right_logical(start, 7)
-        off = start & 127
-        rows = pl.ds(pl.multiple_of(ch * 8, 8), 8)
-        last = low_lane >= off
-        r = [pow_ref[base + k, rows, :] for k in range(19)]
-        for k in range(18):
-            pow2_ref[k, rows, :] = pltpu.roll(jnp.where(last, r[k], r[k + 1]), (128 - off) & 127, 1)
-        return carry
-
-    lax.fori_loop(0, 16, shift, 0, unroll=4)
-    for x in range(4):
-        for w in range(WIN // 128):
-            out_ref[x, :, w * 128 : (w + 1) * 128] = pow2_ref[4 * x + w].astype(bf16)
+    def shift(pair, carry):
+        both = []
+        for e in range(2):
+            ch = 2 * pair + e
+            start = 256 + rate_ref[0, own + ch] * step
+            base = lax.shift_right_logical(start, 7)
+            off = start & 127
+            rows = pl.ds(pl.multiple_of(ch * 8, 8), 8)
+            last = low_lane >= off
+            r = [pow_ref[base + k, rows, :] for k in range(19)]
+            both.append([pltpu.roll(jnp.where(last, r[k], r[k + 1]), (128 - off) & 127, 1) for k in range(18)])
+        rows = pl.ds(pl.multiple_of(pair * 16, 16), 16)
+        tiles = [jnp.concatenate([both[0][k], both[1][k]], axis=0).astype(bf16) for k in range(18)]
+        for x in range(4):
+            for w in range(WIN // 128):
+                out_ref[x, rows, w * 128 : (w + 1) * 128] = tiles[4 * x + w]
+        return carry
+
+    lax.fori_loop(0, 8, shift, 0, unroll=2)
 
 
 def fine(rates, x, first, second, perm):
@@ -285,7 +298,7 @@
             pltpu.VMEM((GRP, 2, 128, 256), bf16),
             pltpu.VMEM((8, 128, 256), bf16),
             pltpu.VMEM((21, 128, 128), f32),
-            pltpu.VMEM((18, 128, 128), f32),
+            pltpu.VMEM((GRP, 128, 128), f32),
             pltpu.SemaphoreType.DMA,
         ],
         compiler_params=pltpu.CompilerParams(vmem_limit_bytes=50 << 20),
@@ -293,29 +306,29 @@
     )(rates, x, first, second, perm)
 
 
-def drift_kernel(x_ref, out_ref, wide_ref, sum_ref):
-    for t in range(STEPS):
-        for w in range(WIN // 128):
-            wide_ref[t, w] = x_ref[t, :, w * 128 : (w + 1) * 128].astype(f32)
-    lane = lax.broadcasted_iota(jnp.int32, (8, 128), 1)
-
-    def body(i, carry):
-        rows = pl.ds(pl.multiple_of(i * 8, 8), 8)
+def drift_kernel(x_ref, out_ref, sum_ref):
+    lane = lax.broadcasted_iota(jnp.int16, (16, 128), 1)
+
+    def body(pair, carry):
+        rows = pl.ds(pl.multiple_of(pair * 16, 16), 16)
         for j in range(NDRIFT):
             acc = None
             for t in range(STEPS):
                 base, off = divmod(j * t, 128)
-                if off == 0:
-                    w = [wide_ref[t, base + k, rows, :] for k in range(4)]
-                else:
-                    r = [wide_ref[t, base + k, rows, :] for k in range(5)]
-                    w = [pltpu.roll(jnp.where(lane >= off, r[k], r[k + 1]), 128 - off, 1) for k in range(4)]
+                r = [x_ref[t, rows, (base + k) * 128 : (base + k + 1) * 128] for k in range(5 if off else 4)]
+                if off:
+                    keep = lane >= jnp.int16(off)
+                    r = [pltpu.roll(jnp.where(keep, r[k], r[k + 1]), 128 - off, 1) for k in range(4)]
+                w = [r[k].astype(f32) for k in range(4)]
                 acc = w if acc is None else [acc[k] + w[k] for k in range(4)]
             for k in range(4):
-                sum_ref[k, pl.ds(i * NDRIFT + j, 8, stride=64), :] = acc[k] * (1.0 / STEPS)
-        return carry
-
-    lax.fori_loop(0, 4, body, 0)
+                done = acc[k] * (1.0 / STEPS)
+                for e in range(2):
+                    at = (2 * pair + e) * NDRIFT + j
+                    sum_ref[k, pl.ds(at, 8, stride=64), :] = done[8 * e : 8 * e + 8]
+        return carry
+
+    lax.fori_loop(0, 2, body, 0)
     for k in range(4):
         out_ref[:, k * 128 : (k + 1) * 128] = sum_ref[k]
 
@@ -327,7 +340,6 @@
         out_specs=pl.BlockSpec(memory_space=pltpu.VMEM),
         out_shape=jax.ShapeDtypeStruct((BEAMS * 64, BINS), f32),
         scratch_shapes=[
-            pltpu.VMEM((STEPS, WIN // 128, 32, 128), f32),
             pltpu.VMEM((4, BEAMS * 64, 128), f32),
         ],
         compiler_params=pltpu.CompilerParams(vmem_limit_bytes=50 << 20),
@@ -341,8 +353,9 @@
     head = lax.slice_in_dim(voltages, 0, 8, axis=2)
     halo = lax.ppermute(head, axes, [(i + 1, i) for i in range(devices - 1)])
     first, second, perm = fine_tables()
-    extra = jnp.stack([busy_mask, drift_low]).astype(f32)
-    small = jnp.concatenate([taps, extra, jnp.zeros((2, N), f32)], axis=0)
+    row = lax.broadcasted_iota(jnp.int32, (8, N), 0)
+    extra = jnp.where(row == TAPS, busy_mask[None, :], drift_low[None, :]).astype(f32)
+    small = jnp.where(row < TAPS, jnp.pad(taps, ((0, 4), (0, 0))), extra)
     wt, rates, tail, filt = front(small, voltages)
     blocks = coarse(tail, halo, small, wt, filt)
     times = lax.all_to_all(blocks, ("zl", "y", "core"), split_axis=0, concat_axis=0, tiled=True)

time: 92.7 us -> 90.1 us (0.972)
  Pallas kernels: 21.1 us -> 18.1 us
  blocking collectives: 64.7 us -> 65.9 us
    pallas_call x1, Pallas kernels: 5.82 us -> 3.62 us  [drift(): pl.pallas_call(drift_kernel, in_specs=[pl.BlockSpec(memory_space=pltpu.VM...]
    all_to_all x1, blocking collectives: 34.5 us -> 35.5 us  [shards(): lax.all_to_all(powers.reshape(16, 32, WIN), ('x', 'zh'), split_axis=0, co...]
  transfers between devices with their start and end apart: 1 -> 1, of which waited for: 0 -> 0; matrix products, arithmetic and copies ran while one was open for 2% -> 1% of each run, Pallas kernels for 7% -> 7%
where the time goes in v4:
time: 90.1 us; the launch traced here: 89.8 us
  blocking collectives  65.9 us (73%)
  Pallas kernels  18.1 us (20%)
  starting transfers between devices  3.91 us (4%)
  local copies, waits for them, and re-layouts  0.98 us (1%)
    all_to_all x1, blocking collectives, shards(): lax.all_to_all(powers.reshape(16, 32, WIN), ('x', 'zh'), split_axis=0, co...  35.5 us
    all_to_all x1, blocking collectives, shards(): lax.all_to_all(blocks, ('zl', 'y', 'core'), split_axis=0, concat_axis=0,...  30.5 us
    pallas_call x1, Pallas kernels, front(): pl.pallas_call(front_kernel, grid=(BEAMS // BPS,), in_specs=[whole((8, N)...  6.01 us
    pallas_call x1, Pallas kernels, coarse(): pl.pallas_call(coarse_kernel, grid=(1,), in_specs=[whole((BEAMS, 4, 8, N)...  4.52 us
    pallas_call x1, Pallas kernels, fine(): pl.pallas_call(fine_kernel, in_specs=[pl.BlockSpec(memory_space=pltpu.SME...  3.94 us
    ppermute x1, starting transfers between devices, shards(): halo = lax.ppermute(head, axes, [(i + 1, i) for i in range(devices - 1)])  3.91 us
    pallas_call x1, Pallas kernels, drift(): pl.pallas_call(drift_kernel, in_specs=[pl.BlockSpec(memory_space=pltpu.VM...  3.62 us
  transfers between devices with their start and end apart: 1, of which 0 were waited for; matrix products, arithmetic and copies ran while one was open for 1% of the time, Pallas kernels for 7%

profile of v4, /device:TPU:32, one launch (start us, length us, event | category | flops | bytes accessed | tf_op | source)
XLA Modules:
  0.0 89.8 jit_solution(10863072771673024693)
XLA Ops:
  0.0 1.0 %slice.3 = bf16[8,4,8,512]{3,2,1,0:T(8,128)(2,1)S(1)} slice(bf16[8,4,128,512]{3,2,1,0:T(8,128)(2,1)} %v_ref.1), slice={[0:8], [0:4], [0:8], [0:512]} | slice | bytes 524288 | tf_op jit(solution)/shard_map/slice | solution.py:353
  1.0 3.9 %collective-permute-start = (bf16[8,4,8,512]{3,2,1,0:T(8,128)(2,1)S(1)}, bf16[8,4,8,512]{3,2,1,0:T(8,128)(2,1)S(1)}, u32[]{:S(2)}, u32[]{:S(2)}) collective-permute-start(bf16[8,4,8,512]{3,2,1,0:T(8,128)(2,1)S(1)} %slice.3), channel_id=1, source_target_pairs={{1,0},{2,1},{3,2},{4,3},{5,4},{6,5},{7,6},{8,7},{9,8},{10,9},{11,1... | collective-permute-start | bytes 786440 | tf_op jit(solution)/shard_map/ppermute | solution.py:354
  4.9 0.8 convert_select_fusion.small_ref.taps_ref
  5.7 6.0 %front.1 = (bf16[16,32,1024]{2,1,0:T(8,128)(2,1)S(1)}, s32[1,256]{1,0:T(1,128)S(1)}, bf16[8,4,8,512]{3,2,1,0:T(8,128)(2,1)S(1)}, bf16[8,256,1024]{2,1,0:T(8,128)(2,1)S(1)}) custom-call(f32[8,512]{1,0:T(8,128)S(1)} %convert_select_fusion.small_ref.taps_ref, bf16[8,4,128,512]{3,2,1,0:T(8,128)(2,1)} %v_ref.1), custom_call_target="tpu_custom_call" | custom-call | tf_op jit(solution)/shard_map/front/pallas_call | solution.py:128
  11.7 0.0 collective-permute-done.halo_ref
  11.7 4.5 %coarse.1 = bf16[16,8,32,256]{3,2,1,0:T(8,128)(2,1)S(1)} custom-call(bf16[8,4,8,512]{3,2,1,0:T(8,128)(2,1)S(1)} %get-tuple-element.10.tail_ref, bf16[8,4,8,512]{3,2,1,0:T(8,128)(2,1)S(1)} %collective-permute-done.halo_ref, f32[8,512]{1,0:T(8,128)S(1)} %convert_select_fusion.small_ref.taps_ref, bf16[16,32,1024]{2,1,0:T(8,128)(2,1)S(1)} %get-tuple-element.11.wt_ref, ...), custom_call_target="tpu_custom_call" | custom-call | tf_op jit(solution)/shard_map/coarse/pallas_call | solution.py:184
  16.3 0.0 copy-start
  16.3 0.0 copy-start.1
  16.3 30.5 %all_to_all.10.x_ref = bf16[16,8,32,256]{3,2,1,0:T(8,128)(2,1)S(1)} all-to-all(bf16[16,8,32,256]{3,2,1,0:T(8,128)(2,1)S(1)} %coarse.1), channel_id=1, replica_groups=mesh['x'=4,'zh'=4,'zl'=2,'y'=4,'core'=2] {'zl','y','core'}, dimensions={0} | all-to-all | bytes 4194304 | tf_op jit(solution)/shard_map/all_to_all | solution.py:361
  46.8 0.0 copy-done
  46.8 0.0 copy-done.1
  46.8 3.9 %fine.1 = bf16[4,128,768]{2,1,0:T(8,128)(2,1)S(1)} custom-call(s32[1,256]{1,0:T(1,128)S(1)} %get-tuple-element.9.rate_ref, bf16[16,8,32,256]{3,2,1,0:T(8,128)(2,1)S(1)} %all_to_all.10.x_ref, bf16[512,512]{1,0:T(8,128)(2,1)S(1)} %copy-done, bf16[16,256,256]{2,1,0:T(8,128)(2,1)} %constant.12.clone.second_hbm, bf16[256,256]{1,0:T(8,128)(2,1)S(1)} %copy-done.1), custom_call_target="tpu_custom_call" | custom-call | tf_op jit(solution)/shard_map/fine/pallas_call | solution.py:285
  50.7 35.5 %all_to_all.11.x_ref = bf16[16,32,768]{2,1,0:T(8,128)(2,1)S(1)} all-to-all(bf16[16,32,768]{2,1,0:T(8,128)(2,1)S(1)} %bitcast.2), channel_id=1, replica_groups=mesh['x'=4,'zh'=4,'zl'=2,'y'=4,'core'=2] {'x','zh'}, dimensions={0} | all-to-all | bytes 1572864 | tf_op jit(solution)/shard_map/all_to_all | solution.py:363
  86.2 3.6 %drift.1 = f32[512,512]{1,0:T(8,128)} custom-call(bf16[16,32,768]{2,1,0:T(8,128)(2,1)S(1)} %all_to_all.11.x_ref), custom_call_target="tpu_custom_call" | custom-call | tf_op jit(solution)/shard_map/drift/pallas_call | solution.py:337
  (1 shorter events, 0.0 us)
Async XLA Ops:
  1.0 10.7 %collective-permute-start = (bf16[8,4,8,512]{3,2,1,0:T(8,128)(2,1)S(1)}, bf16[8,4,8,512]{3,2,1,0:T(8,128)(2,1)S(1)}, u32[]{:S(2)}, u32[]{:S(2)}) collective-permute-start(bf16[8,4,8,512]{3,2,1,0:T(8,128)(2,1)S(1)} %slice.3), channel_id=1, source_target_pairs={{1,0},{2,1},{3,2},{4,3},{5,4},{6,5},{7,6},{8,7},{9,8},{10,9},{11,1... | collective-permute-start | bytes 786440 | tf_op jit(solution)/shard_map/ppermute | solution.py:354
  16.3 30.5 %copy-start = (bf16[512,512]{1,0:T(8,128)(2,1)S(1)}, bf16[512,512]{1,0:T(8,128)(2,1)}, u32[]{:S(2)}) copy-start(bf16[512,512]{1,0:T(8,128)(2,1)} %constant.11.clone.first_ref) | copy-start | bytes 1572868
  16.3 30.5 %copy-start.1 = (bf16[256,256]{1,0:T(8,128)(2,1)S(1)}, bf16[256,256]{1,0:T(8,128)(2,1)}, u32[]{:S(2)}) copy-start(bf16[256,256]{1,0:T(8,128)(2,1)} %constant.13.clone.perm_ref) | copy-start | bytes 393220

commit v5 on v4

--- a/solution.py
+++ b/solution.py
@@ -18,7 +18,6 @@
 GRP = 16
 WIN = 768
 BINS = 512
-BPS = 2
 f32 = jnp.float32
 bf16 = jnp.bfloat16
 
@@ -96,64 +95,64 @@
     rate_ref[...] = rate[0:1].astype(jnp.int32)
 
 
-def front_kernel(small_ref, v_ref, wt_ref, rate_ref, tail_ref, filt_ref, ext_ref, hit_ref):
-    @pl.when(pl.program_id(0) == 0)
-    def _():
-        write_tables(small_ref, wt_ref, rate_ref, hit_ref)
-        for c in range(N // 128):
-            ext_ref[c, BLK : BLK + 8, :] = jnp.zeros((8, 128), f32)
-
-    tail_ref[...] = v_ref[:, :, BLK - 8 : BLK, :]
-
-    def body(bo, carry):
-        b = bo // 4
-        op = bo % 4
-        row = pl.multiple_of((op // 2) * BLK, BLK)
-        for c in range(N // 128):
-            lanes = pl.ds(c * 128, 128)
-            main = v_ref[b, op, :, lanes].astype(f32)
-            ext_ref[c, 0:BLK, :] = main
-            acc = small_ref[0:1, lanes] * main
-            for tap in range(1, TAPS):
-                acc = acc + small_ref[tap : tap + 1, lanes] * ext_ref[c, tap : tap + BLK, :]
-            at = pl.multiple_of((op % 2) * N + c * 128, 128)
-            filt_ref[b, pl.ds(row, BLK), pl.ds(at, 128)] = acc.astype(bf16)
-        return carry
-
-    lax.fori_loop(0, BPS * 4, body, 0, unroll=2)
+def front_kernel(small_ref, v_ref, wt_ref, rate_ref, tail_ref, filt_ref, buf_ref, ext_ref, hit_ref, sem):
+    def fetch(b):
+        return pltpu.make_async_copy(v_ref.at[b], buf_ref.at[b], sem.at[b])
+
+    for b in range(BEAMS):
+        fetch(b).start()
+    write_tables(small_ref, wt_ref, rate_ref, hit_ref)
+    for e in range(2 * N // 128):
+        ext_ref[e, BLK : BLK + 8, :] = jnp.zeros((8, 128), f32)
+
+    def beam(b, carry):
+        fetch(b).wait()
+        tail_ref[b] = buf_ref[b, :, BLK - 8 : BLK, :]
+
+        def body(o, inner):
+            row = pl.multiple_of(o * BLK, BLK)
+            for p in range(2):
+                for c in range(N // 128):
+                    e = p * (N // 128) + c
+                    lanes = pl.ds(c * 128, 128)
+                    main = buf_ref[b, 2 * o + p, :, lanes].astype(f32)
+                    ext_ref[e, 0:BLK, :] = main
+                    acc = small_ref[0:1, lanes] * main
+                    for tap in range(1, TAPS):
+                        acc = acc + small_ref[tap : tap + 1, lanes] * ext_ref[e, tap : tap + BLK, :]
+                    filt_ref[b, pl.ds(row, BLK), e * 128 : (e + 1) * 128] = acc.astype(bf16)
+            return inner
+
+        return lax.fori_loop(0, 2, body, carry)
+
+    lax.fori_loop(0, BEAMS, beam, 0)
 
 
 def front(small, volt):
-    whole = lambda shape: pl.BlockSpec(shape, lambda b: (0,) * len(shape))
+    vmem = pl.BlockSpec(memory_space=pltpu.VMEM)
     return pl.pallas_call(
         front_kernel,
-        grid=(BEAMS // BPS,),
-        in_specs=[whole((8, N)), pl.BlockSpec((BPS, 4, BLK, N), lambda b: (b, 0, 0, 0))],
-        out_specs=(
-            whole((GRP, 32, 2 * N)),
-            whole((1, 256)),
-            pl.BlockSpec((BPS, 4, 8, N), lambda b: (b, 0, 0, 0)),
-            pl.BlockSpec((BPS, 256, 2 * N), lambda b: (b, 0, 0)),
-        ),
+        in_specs=[vmem, pl.BlockSpec(memory_space=pltpu.HBM)],
+        out_specs=(vmem,) * 4,
         out_shape=(
             jax.ShapeDtypeStruct((GRP, 32, 2 * N), bf16),
             jax.ShapeDtypeStruct((1, 256), jnp.int32),
             jax.ShapeDtypeStruct((BEAMS, 4, 8, N), bf16),
             jax.ShapeDtypeStruct((BEAMS, 256, 2 * N), bf16),
         ),
-        scratch_shapes=[pltpu.VMEM((N // 128, BLK + 8, 128), f32), pltpu.VMEM((256, N), bf16)],
+        scratch_shapes=[
+            pltpu.VMEM((BEAMS, 4, BLK, N), bf16),
+            pltpu.VMEM((2 * N // 128, BLK + 8, 128), f32),
+            pltpu.VMEM((256, N), bf16),
+            pltpu.SemaphoreType.DMA((BEAMS,)),
+        ],
         compiler_params=pltpu.CompilerParams(vmem_limit_bytes=46 << 20),
         name="front",
     )(small, volt)
 
 
-def coarse_kernel(tail_ref, halo_ref, taps_ref, wt_ref, filt_ref, out_ref, buf_ref, ext_ref, res_ref, in_sem, out_sem):
-    fetch = [pltpu.make_async_copy(filt_ref.at[b], buf_ref.at[b], in_sem.at[b]) for b in range(BEAMS)]
-    send = [pltpu.make_async_copy(res_ref.at[b], out_ref.at[:, b], out_sem.at[b]) for b in range(BEAMS)]
-    for copy in fetch:
-        copy.start()
+def coarse_kernel(tail_ref, halo_ref, small_ref, wt_ref, filt_ref, out_ref, buf_ref, ext_ref):
     for b in range(BEAMS):
-        fetch[b].wait()
         for op in range(4):
             o, p = divmod(op, 2)
             for c in range(N // 128):
@@ -161,9 +160,9 @@
                 slot = (b % 2) * 16 + op * 4 + c
                 ext_ref[slot, 0:8, :] = tail_ref[b, op, :, lanes].astype(f32)
                 ext_ref[slot, 8:16, :] = halo_ref[b, op, :, lanes].astype(f32)
-                acc = taps_ref[0:1, lanes] * ext_ref[slot, 0:8, :]
+                acc = small_ref[0:1, lanes] * ext_ref[slot, 0:8, :]
                 for tap in range(1, TAPS):
-                    acc = acc + taps_ref[tap : tap + 1, lanes] * ext_ref[slot, tap : tap + 8, :]
+                    acc = acc + small_ref[tap : tap + 1, lanes] * ext_ref[slot, tap : tap + 8, :]
                 buf_ref[b, (o + 1) * BLK - 8 : (o + 1) * BLK, p * N + c * 128 : p * N + (c + 1) * 128] = acc.astype(bf16)
         for h in range(2):
             half = slice(h * GRP // 2, (h + 1) * GRP // 2)
@@ -173,33 +172,21 @@
                 (((1,), (1,)), ((), ())),
                 preferred_element_type=f32,
             )
-            res_ref[b, half] = (res * (N ** -0.5)).astype(bf16).reshape(GRP // 2, 32, 256)
-        send[b].start()
-    for copy in send:
-        copy.wait()
+            out_ref[half, b] = (res * (N ** -0.5)).astype(bf16).reshape(GRP // 2, 32, 256)
 
 
 def coarse(tail, halo, small, wt, filt):
-    whole = lambda shape: pl.BlockSpec(shape, lambda b: (0,) * len(shape))
+    vmem = pl.BlockSpec(memory_space=pltpu.VMEM)
     return pl.pallas_call(
         coarse_kernel,
-        grid=(1,),
-        in_specs=[
-            whole((BEAMS, 4, 8, N)),
-            whole((BEAMS, 4, 8, N)),
-            whole((8, N)),
-            whole((GRP, 32, 2 * N)),
-            pl.BlockSpec(memory_space=pltpu.HBM),
-        ],
-        out_specs=pl.BlockSpec(memory_space=pltpu.HBM),
-        out_shape=jax.ShapeDtypeStruct((GRP, BEAMS, 32, 256), bf16),
-        scratch_shapes=[
-            pltpu.VMEM((BEAMS, 256, 2 * N), bf16),
-            pltpu.VMEM((32, 16, 128), f32),
-            pltpu.VMEM((BEAMS, GRP, 32, 256), bf16),
-            pltpu.SemaphoreType.DMA((BEAMS,)),
-            pltpu.SemaphoreType.DMA((BEAMS,)),
-        ],
+        in_specs=[vmem] * 5,
+        out_specs=(vmem, vmem),
+        out_shape=(
+            jax.ShapeDtypeStruct((GRP, BEAMS, 32, 256), bf16),
+            jax.ShapeDtypeStruct((BEAMS, 256, 2 * N), bf16),
+        ),
+        input_output_aliases={4: 1},
+        scratch_shapes=[pltpu.VMEM((32, 16, 128), f32)],
         compiler_params=pltpu.CompilerParams(vmem_limit_bytes=46 << 20),
         name="coarse",
     )(tail, halo, small, wt, filt)
@@ -357,7 +344,7 @@
     extra = jnp.where(row == TAPS, busy_mask[None, :], drift_low[None, :]).astype(f32)
     small = jnp.where(row < TAPS, jnp.pad(taps, ((0, 4), (0, 0))), extra)
     wt, rates, tail, filt = front(small, voltages)
-    blocks = coarse(tail, halo, small, wt, filt)
+    blocks, _ = coarse(tail, halo, small, wt, filt)
     times = lax.all_to_all(blocks, ("zl", "y", "core"), split_axis=0, concat_axis=0, tiled=True)
     powers = fine(rates, times, jnp.asarray(first), jnp.asarray(second), jnp.asarray(perm))
     wins = lax.all_to_all(powers.reshape(16, 32, WIN), ("x", "zh"), split_axis=0, concat_axis=0, tiled=True)

time: 90.1 us -> 87.8 us (0.974)
  Pallas kernels: 18.1 us -> 14.6 us
  blocking collectives: 65.9 us -> 67.1 us
    pallas_call x2, Pallas kernels: 10.5 us -> 7.07 us  [the longest x1 4.67 us: front(): pl.pallas_call(front_kernel, in_specs=[vmem, pl.BlockSpec(memory_space=pl...]
    all_to_all x1, blocking collectives: 30.5 us -> 31.7 us  [shards(): lax.all_to_all(blocks, ('zl', 'y', 'core'), split_axis=0, concat_axis=0,...]
  transfers between devices with their start and end apart: 1 -> 1, of which waited for: 0 -> 0; matrix products, arithmetic and copies ran while one was open for 1% -> 1% of each run, Pallas kernels for 7% -> 5%
where the time goes in v5:
time: 87.8 us; the launch traced here: 87.5 us
  blocking collectives  67.1 us (76%)
  Pallas kernels  14.6 us (17%)
  starting transfers between devices  3.91 us (4%)
  local copies, waits for them, and re-layouts  0.98 us (1%)
    all_to_all x1, blocking collectives, shards(): lax.all_to_all(powers.reshape(16, 32, WIN), ('x', 'zh'), split_axis=0, co...  35.5 us
    all_to_all x1, blocking collectives, shards(): lax.all_to_all(blocks, ('zl', 'y', 'core'), split_axis=0, concat_axis=0,...  31.7 us
    pallas_call x1, Pallas kernels, front(): pl.pallas_call(front_kernel, in_specs=[vmem, pl.BlockSpec(memory_space=pl...  4.67 us
    pallas_call x1, Pallas kernels, fine(): pl.pallas_call(fine_kernel, in_specs=[pl.BlockSpec(memory_space=pltpu.SME...  3.94 us
    ppermute x1, starting transfers between devices, shards(): halo = lax.ppermute(head, axes, [(i + 1, i) for i in range(devices - 1)])  3.91 us
    pallas_call x1, Pallas kernels, drift(): pl.pallas_call(drift_kernel, in_specs=[pl.BlockSpec(memory_space=pltpu.VM...  3.62 us
    pallas_call x1, Pallas kernels, coarse(): pl.pallas_call(coarse_kernel, in_specs=[vmem] * 5, out_specs=(vmem, vmem)...  2.4 us
  transfers between devices with their start and end apart: 1, of which 0 were waited for; matrix products, arithmetic and copies ran while one was open for 1% of the time, Pallas kernels for 5%

profile of v5, /device:TPU:32, one launch (start us, length us, event | category | flops | bytes accessed | tf_op | source)
XLA Modules:
  0.0 87.5 jit_solution(2426477953082728010)
XLA Ops:
  0.0 1.0 %slice.3 = bf16[8,4,8,512]{3,2,1,0:T(8,128)(2,1)S(1)} slice(bf16[8,4,128,512]{3,2,1,0:T(8,128)(2,1)} %v_ref.1), slice={[0:8], [0:4], [0:8], [0:512]} | slice | bytes 524288 | tf_op jit(solution)/shard_map/slice | solution.py:340
  1.0 3.9 %collective-permute-start = (bf16[8,4,8,512]{3,2,1,0:T(8,128)(2,1)S(1)}, bf16[8,4,8,512]{3,2,1,0:T(8,128)(2,1)S(1)}, u32[]{:S(2)}, u32[]{:S(2)}) collective-permute-start(bf16[8,4,8,512]{3,2,1,0:T(8,128)(2,1)S(1)} %slice.3), channel_id=1, source_target_pairs={{1,0},{2,1},{3,2},{4,3},{5,4},{6,5},{7,6},{8,7},{9,8},{10,9},{11,1... | collective-permute-start | bytes 786440 | tf_op jit(solution)/shard_map/ppermute | solution.py:341
  4.9 0.8 convert_select_fusion.small_ref
  5.7 4.7 %front.1 = (bf16[16,32,1024]{2,1,0:T(8,128)(2,1)S(1)}, s32[1,256]{1,0:T(1,128)S(1)}, bf16[8,4,8,512]{3,2,1,0:T(8,128)(2,1)S(1)}, bf16[8,256,1024]{2,1,0:T(8,128)(2,1)S(1)}) custom-call(f32[8,512]{1,0:T(8,128)S(1)} %convert_select_fusion.small_ref, bf16[8,4,128,512]{3,2,1,0:T(8,128)(2,1)} %v_ref.1), custom_call_target="tpu_custom_call" | custom-call | tf_op jit(solution)/shard_map/front/pallas_call | solution.py:133
  10.4 0.0 collective-permute-done.halo_ref
  10.4 0.0 copy-start
  10.4 0.0 copy-start.1
  10.4 2.4 %coarse.1 = (bf16[16,8,32,256]{3,2,1,0:T(8,128)(2,1)S(1)}, bf16[8,256,1024]{2,1,0:T(8,128)(2,1)S(1)}) custom-call(bf16[8,4,8,512]{3,2,1,0:T(8,128)(2,1)S(1)} %get-tuple-element.11.tail_ref, bf16[8,4,8,512]{3,2,1,0:T(8,128)(2,1)S(1)} %collective-permute-done.halo_ref, f32[8,512]{1,0:T(8,128)S(1)} %convert_select_fusion.small_ref, ...), custom_call_target="tpu_custom_call", output_to_operand_aliasing={{1}: (4, {})} | custom-call | tf_op jit(solution)/shard_map/coarse/pallas_call | solution.py:180
  12.8 31.7 %all_to_all.10.x_ref = bf16[16,8,32,256]{3,2,1,0:T(8,128)(2,1)S(1)} all-to-all(bf16[16,8,32,256]{3,2,1,0:T(8,128)(2,1)S(1)} %get-tuple-element.14), channel_id=1, replica_groups=mesh['x'=4,'zh'=4,'zl'=2,'y'=4,'core'=2] {'zl','y','core'}, dimensions={0} | all-to-all | bytes 4194304 | tf_op jit(solution)/shard_map/all_to_all | solution.py:348
  44.5 0.0 copy-done
  44.5 0.0 copy-done.1
  44.5 3.9 %fine.1 = bf16[4,128,768]{2,1,0:T(8,128)(2,1)S(1)} custom-call(s32[1,256]{1,0:T(1,128)S(1)} %get-tuple-element.10.rate_ref, bf16[16,8,32,256]{3,2,1,0:T(8,128)(2,1)S(1)} %all_to_all.10.x_ref, bf16[512,512]{1,0:T(8,128)(2,1)S(1)} %copy-done, bf16[16,256,256]{2,1,0:T(8,128)(2,1)} %constant.12.clone.second_hbm, bf16[256,256]{1,0:T(8,128)(2,1)S(1)} %copy-done.1), custom_call_target="tpu_custom_call" | custom-call | tf_op jit(solution)/shard_map/fine/pallas_call | solution.py:272
  48.5 35.5 %all_to_all.11.x_ref = bf16[16,32,768]{2,1,0:T(8,128)(2,1)S(1)} all-to-all(bf16[16,32,768]{2,1,0:T(8,128)(2,1)S(1)} %bitcast.2), channel_id=1, replica_groups=mesh['x'=4,'zh'=4,'zl'=2,'y'=4,'core'=2] {'x','zh'}, dimensions={0} | all-to-all | bytes 1572864 | tf_op jit(solution)/shard_map/all_to_all | solution.py:350
  83.9 3.6 %drift.1 = f32[512,512]{1,0:T(8,128)} custom-call(bf16[16,32,768]{2,1,0:T(8,128)(2,1)S(1)} %all_to_all.11.x_ref), custom_call_target="tpu_custom_call" | custom-call | tf_op jit(solution)/shard_map/drift/pallas_call | solution.py:324
  (1 shorter events, 0.0 us)
Async XLA Ops:
  1.0 9.4 %collective-permute-start = (bf16[8,4,8,512]{3,2,1,0:T(8,128)(2,1)S(1)}, bf16[8,4,8,512]{3,2,1,0:T(8,128)(2,1)S(1)}, u32[]{:S(2)}, u32[]{:S(2)}) collective-permute-start(bf16[8,4,8,512]{3,2,1,0:T(8,128)(2,1)S(1)} %slice.3), channel_id=1, source_target_pairs={{1,0},{2,1},{3,2},{4,3},{5,4},{6,5},{7,6},{8,7},{9,8},{10,9},{11,1... | collective-permute-start | bytes 786440 | tf_op jit(solution)/shard_map/ppermute | solution.py:341
  10.4 34.1 %copy-start = (bf16[512,512]{1,0:T(8,128)(2,1)S(1)}, bf16[512,512]{1,0:T(8,128)(2,1)}, u32[]{:S(2)}) copy-start(bf16[512,512]{1,0:T(8,128)(2,1)} %constant.11.clone.first_ref) | copy-start | bytes 1572868
  10.4 34.1 %copy-start.1 = (bf16[256,256]{1,0:T(8,128)(2,1)S(1)}, bf16[256,256]{1,0:T(8,128)(2,1)}, u32[]{:S(2)}) copy-start(bf16[256,256]{1,0:T(8,128)(2,1)} %constant.13.clone.perm_ref) | copy-start | bytes 393220

commit v6 on v5

--- a/solution.py
+++ b/solution.py
@@ -9,6 +9,7 @@
 from jax.sharding import Mesh, PartitionSpec as P
 
 TAPS = 4
+HALO = 4
 NDRIFT = 16
 N = 512
 FINE = 2048
@@ -159,7 +160,7 @@
                 lanes = pl.ds(c * 128, 128)
                 slot = (b % 2) * 16 + op * 4 + c
                 ext_ref[slot, 0:8, :] = tail_ref[b, op, :, lanes].astype(f32)
-                ext_ref[slot, 8:16, :] = halo_ref[b, op, :, lanes].astype(f32)
+                ext_ref[slot, 8 : 8 + HALO, :] = halo_ref[b, op, :, lanes].astype(f32)
                 acc = small_ref[0:1, lanes] * ext_ref[slot, 0:8, :]
                 for tap in range(1, TAPS):
                     acc = acc + small_ref[tap : tap + 1, lanes] * ext_ref[slot, tap : tap + 8, :]
@@ -257,11 +258,11 @@
             last = low_lane >= off
             r = [pow_ref[base + k, rows, :] for k in range(19)]
             both.append([pltpu.roll(jnp.where(last, r[k], r[k + 1]), (128 - off) & 127, 1) for k in range(18)])
-        rows = pl.ds(pl.multiple_of(pair * 16, 16), 16)
+        rows = pl.ds(pl.multiple_of((pair % 2) * 16, 16), 16)
         tiles = [jnp.concatenate([both[0][k], both[1][k]], axis=0).astype(bf16) for k in range(18)]
         for x in range(4):
             for w in range(WIN // 128):
-                out_ref[x, rows, w * 128 : (w + 1) * 128] = tiles[4 * x + w]
+                out_ref[pair // 2, x, rows, w * 128 : (w + 1) * 128] = tiles[4 * x + w]
         return carry
 
     lax.fori_loop(0, 8, shift, 0, unroll=2)
@@ -279,7 +280,7 @@
             vmem,
         ],
         out_specs=vmem,
-        out_shape=jax.ShapeDtypeStruct((4, 128, WIN), bf16),
+        out_shape=jax.ShapeDtypeStruct((4, 4, 32, WIN), bf16),
         scratch_shapes=[
             pltpu.VMEM((GRP, 256, 256), bf16),
             pltpu.VMEM((GRP, 2, 128, 256), bf16),
@@ -293,8 +294,12 @@
     )(rates, x, first, second, perm)
 
 
-def drift_kernel(x_ref, out_ref, sum_ref):
+def drift_kernel(x_ref, out_ref, sum_ref, stage_ref, sem):
     lane = lax.broadcasted_iota(jnp.int16, (16, 128), 1)
+
+    def send(b, pair):
+        part = pl.ds(pl.multiple_of(b * 64 + pair * 32, 32), 32)
+        return pltpu.make_async_copy(stage_ref.at[part], out_ref.at[part], sem.at[pair, b])
 
     def body(pair, carry):
         rows = pl.ds(pl.multiple_of(pair * 16, 16), 16)
@@ -302,7 +307,7 @@
             acc = None
             for t in range(STEPS):
                 base, off = divmod(j * t, 128)
-                r = [x_ref[t, rows, (base + k) * 128 : (base + k + 1) * 128] for k in range(5 if off else 4)]
+                r = [x_ref[t % 4 * 4 + t // 4, rows, (base + k) * 128 : (base + k + 1) * 128] for k in range(5 if off else 4)]
                 if off:
                     keep = lane >= jnp.int16(off)
                     r = [pltpu.roll(jnp.where(keep, r[k], r[k + 1]), 128 - off, 1) for k in range(4)]
@@ -313,21 +318,29 @@
                 for e in range(2):
                     at = (2 * pair + e) * NDRIFT + j
                     sum_ref[k, pl.ds(at, 8, stride=64), :] = done[8 * e : 8 * e + 8]
+        for b in range(BEAMS):
+            part = pl.ds(pl.multiple_of(b * 64 + pair * 32, 32), 32)
+            for k in range(4):
+                stage_ref[part, k * 128 : (k + 1) * 128] = sum_ref[k, part, :]
+            send(b, pair).start()
         return carry
 
     lax.fori_loop(0, 2, body, 0)
-    for k in range(4):
-        out_ref[:, k * 128 : (k + 1) * 128] = sum_ref[k]
+    for pair in range(2):
+        for b in range(BEAMS):
+            send(b, pair).wait()
 
 
 def drift(x):
     return pl.pallas_call(
         drift_kernel,
         in_specs=[pl.BlockSpec(memory_space=pltpu.VMEM)],
-        out_specs=pl.BlockSpec(memory_space=pltpu.VMEM),
+        out_specs=pl.BlockSpec(memory_space=pltpu.HBM),
         out_shape=jax.ShapeDtypeStruct((BEAMS * 64, BINS), f32),
         scratch_shapes=[
             pltpu.VMEM((4, BEAMS * 64, 128), f32),
+            pltpu.VMEM((BEAMS * 64, BINS), f32),
+            pltpu.SemaphoreType.DMA((2, BEAMS)),
         ],
         compiler_params=pltpu.CompilerParams(vmem_limit_bytes=50 << 20),
         name="drift",
@@ -337,7 +350,7 @@
 def shards(voltages, taps, busy_mask, drift_low):
     axes = ("x", "zh", "zl", "y", "core")
     devices = lax.axis_size(axes)
-    head = lax.slice_in_dim(voltages, 0, 8, axis=2)
+    head = lax.slice_in_dim(voltages, 0, HALO, axis=2)
     halo = lax.ppermute(head, axes, [(i + 1, i) for i in range(devices - 1)])
     first, second, perm = fine_tables()
     row = lax.broadcasted_iota(jnp.int32, (8, N), 0)
@@ -347,7 +360,7 @@
     blocks, _ = coarse(tail, halo, small, wt, filt)
     times = lax.all_to_all(blocks, ("zl", "y", "core"), split_axis=0, concat_axis=0, tiled=True)
     powers = fine(rates, times, jnp.asarray(first), jnp.asarray(second), jnp.asarray(perm))
-    wins = lax.all_to_all(powers.reshape(16, 32, WIN), ("x", "zh"), split_axis=0, concat_axis=0, tiled=True)
+    wins = lax.all_to_all(powers.reshape(16, 32, WIN), ("zh", "x"), split_axis=0, concat_axis=0, tiled=True)
     out = drift(wins)
     return out.reshape(BEAMS, 4, NDRIFT, BINS)
 

time: 87.8 us -> 86 us (0.979)
  blocking collectives: 67.1 us -> 65.4 us
    all_to_all x1, blocking collectives: 31.7 us -> 30.2 us  [shards(): lax.all_to_all(blocks, ('zl', 'y', 'core'), split_axis=0, concat_axis=0,...]
  transfers between devices with their start and end apart: 1 -> 1, of which waited for: 0 -> 0; matrix products, arithmetic and copies ran while one was open for 1% -> 1% of each run, Pallas kernels for 5% -> 6%
where the time goes in v6:
time: 86 us; the launch traced here: 85.8 us
  blocking collectives  65.4 us (76%)
  Pallas kernels  14.6 us (17%)
  starting transfers between devices  3.91 us (5%)
  local copies, waits for them, and re-layouts  1 us (1%)
    all_to_all x1, blocking collectives, shards(): lax.all_to_all(powers.reshape(16, 32, WIN), ('zh', 'x'), split_axis=0, co...  35.2 us
    all_to_all x1, blocking collectives, shards(): lax.all_to_all(blocks, ('zl', 'y', 'core'), split_axis=0, concat_axis=0,...  30.2 us
    pallas_call x1, Pallas kernels, front(): pl.pallas_call(front_kernel, in_specs=[vmem, pl.BlockSpec(memory_space=pl...  4.75 us
    pallas_call x1, Pallas kernels, fine(): pl.pallas_call(fine_kernel, in_specs=[pl.BlockSpec(memory_space=pltpu.SME...  3.94 us
    ppermute x1, starting transfers between devices, shards(): halo = lax.ppermute(head, axes, [(i + 1, i) for i in range(devices - 1)])  3.91 us
    pallas_call x1, Pallas kernels, drift(): pl.pallas_call(drift_kernel, in_specs=[pl.BlockSpec(memory_space=pltpu.VM...  3.46 us
    pallas_call x1, Pallas kernels, coarse(): pl.pallas_call(coarse_kernel, in_specs=[vmem] * 5, out_specs=(vmem, vmem)...  2.41 us
  transfers between devices with their start and end apart: 1, of which 0 were waited for; matrix products, arithmetic and copies ran while one was open for 1% of the time, Pallas kernels for 6%

profile of v6, /device:TPU:32, one launch (start us, length us, event | category | flops | bytes accessed | tf_op | source)
XLA Modules:
  0.0 85.8 jit_solution(17323099640822315654)
XLA Ops:
  0.0 1.0 %slice.3 = bf16[8,4,4,512]{3,2,1,0:T(4,128)(2,1)S(1)} slice(bf16[8,4,128,512]{3,2,1,0:T(8,128)(2,1)} %v_ref.1), slice={[0:8], [0:4], [0:4], [0:512]} | slice | bytes 262144 | tf_op jit(solution)/shard_map/slice | solution.py:353
  1.0 3.9 %collective-permute-start = (bf16[8,4,4,512]{3,2,1,0:T(4,128)(2,1)S(1)}, bf16[8,4,4,512]{3,2,1,0:T(4,128)(2,1)S(1)}, u32[]{:S(2)}, u32[]{:S(2)}) collective-permute-start(bf16[8,4,4,512]{3,2,1,0:T(4,128)(2,1)S(1)} %slice.3), channel_id=1, source_target_pairs={{1,0},{2,1},{3,2},{4,3},{5,4},{6,5},{7,6},{8,7},{9,8},{10,9},{11,1... | collective-permute-start | bytes 393224 | tf_op jit(solution)/shard_map/ppermute | solution.py:354
  4.9 0.8 convert_select_fusion.small_ref
  5.7 4.8 %front.1 = (bf16[16,32,1024]{2,1,0:T(8,128)(2,1)S(1)}, s32[1,256]{1,0:T(1,128)S(1)}, bf16[8,4,8,512]{3,2,1,0:T(8,128)(2,1)S(1)}, bf16[8,256,1024]{2,1,0:T(8,128)(2,1)S(1)}) custom-call(f32[8,512]{1,0:T(8,128)S(1)} %convert_select_fusion.small_ref, bf16[8,4,128,512]{3,2,1,0:T(8,128)(2,1)} %v_ref.1), custom_call_target="tpu_custom_call" | custom-call | tf_op jit(solution)/shard_map/front/pallas_call | solution.py:134
  10.5 0.0 collective-permute-done.halo_ref
  10.5 0.0 copy-start
  10.5 0.0 copy-start.1
  10.5 2.4 %coarse.1 = (bf16[16,8,32,256]{3,2,1,0:T(8,128)(2,1)S(1)}, bf16[8,256,1024]{2,1,0:T(8,128)(2,1)S(1)}) custom-call(bf16[8,4,8,512]{3,2,1,0:T(8,128)(2,1)S(1)} %get-tuple-element.11.tail_ref, bf16[8,4,4,512]{3,2,1,0:T(4,128)(2,1)S(1)} %collective-permute-done.halo_ref, f32[8,512]{1,0:T(8,128)S(1)} %convert_select_fusion.small_ref, ...), custom_call_target="tpu_custom_call", output_to_operand_aliasing={{1}: (4, {})} | custom-call | tf_op jit(solution)/shard_map/coarse/pallas_call | solution.py:181
  12.9 30.2 %all_to_all.10.x_ref = bf16[16,8,32,256]{3,2,1,0:T(8,128)(2,1)S(1)} all-to-all(bf16[16,8,32,256]{3,2,1,0:T(8,128)(2,1)S(1)} %get-tuple-element.14), channel_id=1, replica_groups=mesh['x'=4,'zh'=4,'zl'=2,'y'=4,'core'=2] {'zl','y','core'}, dimensions={0} | all-to-all | bytes 4194304 | tf_op jit(solution)/shard_map/all_to_all | solution.py:361
  43.1 0.0 copy-done
  43.1 0.0 copy-done.1
  43.1 3.9 %fine.1 = bf16[4,4,32,768]{3,2,1,0:T(8,128)(2,1)S(1)} custom-call(s32[1,256]{1,0:T(1,128)S(1)} %get-tuple-element.10.rate_ref, bf16[16,8,32,256]{3,2,1,0:T(8,128)(2,1)S(1)} %all_to_all.10.x_ref, bf16[512,512]{1,0:T(8,128)(2,1)S(1)} %copy-done, bf16[16,256,256]{2,1,0:T(8,128)(2,1)} %constant.12.clone.second_hbm, bf16[256,256]{1,0:T(8,128)(2,1)S(1)} %copy-done.1), custom_call_target="tpu_custom_call" | custom-call | tf_op jit(solution)/shard_map/fine/pallas_call | solution.py:273
  47.1 35.2 %all_to_all.11.x_ref = bf16[16,32,768]{2,1,0:T(8,128)(2,1)S(1)} all-to-all(bf16[16,32,768]{2,1,0:T(8,128)(2,1)S(1)} %bitcast.2), channel_id=1, replica_groups=mesh['x'=4,'zh'=4,'zl'=2,'y'=4,'core'=2] {'zh','x'}, dimensions={0} | all-to-all | bytes 1572864 | tf_op jit(solution)/shard_map/all_to_all | solution.py:363
  82.3 3.5 %drift.1 = f32[512,512]{1,0:T(8,128)} custom-call(bf16[16,32,768]{2,1,0:T(8,128)(2,1)S(1)} %all_to_all.11.x_ref), custom_call_target="tpu_custom_call" | custom-call | tf_op jit(solution)/shard_map/drift/pallas_call | solution.py:335
  (1 shorter events, 0.0 us)
Async XLA Ops:
  1.0 9.5 %collective-permute-start = (bf16[8,4,4,512]{3,2,1,0:T(4,128)(2,1)S(1)}, bf16[8,4,4,512]{3,2,1,0:T(4,128)(2,1)S(1)}, u32[]{:S(2)}, u32[]{:S(2)}) collective-permute-start(bf16[8,4,4,512]{3,2,1,0:T(4,128)(2,1)S(1)} %slice.3), channel_id=1, source_target_pairs={{1,0},{2,1},{3,2},{4,3},{5,4},{6,5},{7,6},{8,7},{9,8},{10,9},{11,1... | collective-permute-start | bytes 393224 | tf_op jit(solution)/shard_map/ppermute | solution.py:354
  10.5 32.6 %copy-start = (bf16[512,512]{1,0:T(8,128)(2,1)S(1)}, bf16[512,512]{1,0:T(8,128)(2,1)}, u32[]{:S(2)}) copy-start(bf16[512,512]{1,0:T(8,128)(2,1)} %constant.11.clone.first_ref) | copy-start | bytes 1572868
  10.5 32.6 %copy-start.1 = (bf16[256,256]{1,0:T(8,128)(2,1)S(1)}, bf16[256,256]{1,0:T(8,128)(2,1)}, u32[]{:S(2)}) copy-start(bf16[256,256]{1,0:T(8,128)(2,1)} %constant.13.clone.perm_ref) | copy-start | bytes 393220

commit v7 on v6

--- a/solution.py
+++ b/solution.py
@@ -124,7 +124,7 @@
                     filt_ref[b, pl.ds(row, BLK), e * 128 : (e + 1) * 128] = acc.astype(bf16)
             return inner
 
-        return lax.fori_loop(0, 2, body, carry)
+        return lax.fori_loop(0, 2, body, carry, unroll=2)
 
     lax.fori_loop(0, BEAMS, beam, 0)
 
@@ -209,7 +209,7 @@
                         lhs_ref[8 * h + f, o, rows, q * BLK : (q + 1) * BLK] = part[:, o * BLK : (o + 1) * BLK]
         return carry
 
-    lax.fori_loop(0, BEAMS, beam, 0, unroll=4)
+    lax.fori_loop(0, BEAMS, beam, 0, unroll=8)
     load.wait()
     for f in range(GRP):
         total = None
@@ -231,7 +231,7 @@
                 mix_ref[(8 - m) % 8, rows, h * 128 : (h + 1) * 128] = v[m].astype(bf16)
         return carry
 
-    lax.fori_loop(0, BEAMS, mix, 0, unroll=2)
+    lax.fori_loop(0, BEAMS, mix, 0, unroll=4)
     zero = jnp.zeros((128, 128), f32)
     for e in (0, 1, 18, 19, 20):
         pow_ref[e] = zero
@@ -265,7 +265,7 @@
                 out_ref[pair // 2, x, rows, w * 128 : (w + 1) * 128] = tiles[4 * x + w]
         return carry
 
-    lax.fori_loop(0, 8, shift, 0, unroll=2)
+    lax.fori_loop(0, 8, shift, 0, unroll=4)
 
 
 def fine(rates, x, first, second, perm):

time: 86 us -> 85.9 us (level)
  no operation moved by 1% of the time
where the time goes in v7:
time: 85.9 us; the launch traced here: 85.6 us
  blocking collectives  65.5 us (76%)
  Pallas kernels  14.4 us (17%)
  starting transfers between devices  3.91 us (5%)
  local copies, waits for them, and re-layouts  1 us (1%)
    all_to_all x1, blocking collectives, shards(): lax.all_to_all(powers.reshape(16, 32, WIN), ('zh', 'x'), split_axis=0, co...  35.2 us
    all_to_all x1, blocking collectives, shards(): lax.all_to_all(blocks, ('zl', 'y', 'core'), split_axis=0, concat_axis=0,...  30.2 us
    pallas_call x1, Pallas kernels, front(): pl.pallas_call(front_kernel, in_specs=[vmem, pl.BlockSpec(memory_space=pl...  4.72 us
    ppermute x1, starting transfers between devices, shards(): halo = lax.ppermute(head, axes, [(i + 1, i) for i in range(devices - 1)])  3.91 us
    pallas_call x1, Pallas kernels, fine(): pl.pallas_call(fine_kernel, in_specs=[pl.BlockSpec(memory_space=pltpu.SME...  3.77 us
    pallas_call x1, Pallas kernels, drift(): pl.pallas_call(drift_kernel, in_specs=[pl.BlockSpec(memory_space=pltpu.VM...  3.46 us
    pallas_call x1, Pallas kernels, coarse(): pl.pallas_call(coarse_kernel, in_specs=[vmem] * 5, out_specs=(vmem, vmem)...  2.41 us
  transfers between devices with their start and end apart: 1, of which 0 were waited for; matrix products, arithmetic and copies ran while one was open for 1% of the time, Pallas kernels for 6%

profile of v7, /device:TPU:32, one launch (start us, length us, event | category | flops | bytes accessed | tf_op | source)
XLA Modules:
  0.0 85.6 jit_solution(6190995814005246280)
XLA Ops:
  0.0 1.0 %slice.3 = bf16[8,4,4,512]{3,2,1,0:T(4,128)(2,1)S(1)} slice(bf16[8,4,128,512]{3,2,1,0:T(8,128)(2,1)} %v_ref.1), slice={[0:8], [0:4], [0:4], [0:512]} | slice | bytes 262144 | tf_op jit(solution)/shard_map/slice | solution.py:353
  1.0 3.9 %collective-permute-start = (bf16[8,4,4,512]{3,2,1,0:T(4,128)(2,1)S(1)}, bf16[8,4,4,512]{3,2,1,0:T(4,128)(2,1)S(1)}, u32[]{:S(2)}, u32[]{:S(2)}) collective-permute-start(bf16[8,4,4,512]{3,2,1,0:T(4,128)(2,1)S(1)} %slice.3), channel_id=1, source_target_pairs={{1,0},{2,1},{3,2},{4,3},{5,4},{6,5},{7,6},{8,7},{9,8},{10,9},{11,1... | collective-permute-start | bytes 393224 | tf_op jit(solution)/shard_map/ppermute | solution.py:354
  4.9 0.8 convert_select_fusion.small_ref
  5.7 4.7 %front.1 = (bf16[16,32,1024]{2,1,0:T(8,128)(2,1)S(1)}, s32[1,256]{1,0:T(1,128)S(1)}, bf16[8,4,8,512]{3,2,1,0:T(8,128)(2,1)S(1)}, bf16[8,256,1024]{2,1,0:T(8,128)(2,1)S(1)}) custom-call(f32[8,512]{1,0:T(8,128)S(1)} %convert_select_fusion.small_ref, bf16[8,4,128,512]{3,2,1,0:T(8,128)(2,1)} %v_ref.1), custom_call_target="tpu_custom_call" | custom-call | tf_op jit(solution)/shard_map/front/pallas_call | solution.py:134
  10.4 0.0 collective-permute-done.halo_ref
  10.4 0.0 copy-start
  10.5 0.0 copy-start.1
  10.5 2.4 %coarse.1 = (bf16[16,8,32,256]{3,2,1,0:T(8,128)(2,1)S(1)}, bf16[8,256,1024]{2,1,0:T(8,128)(2,1)S(1)}) custom-call(bf16[8,4,8,512]{3,2,1,0:T(8,128)(2,1)S(1)} %get-tuple-element.11.tail_ref, bf16[8,4,4,512]{3,2,1,0:T(4,128)(2,1)S(1)} %collective-permute-done.halo_ref, f32[8,512]{1,0:T(8,128)S(1)} %convert_select_fusion.small_ref, ...), custom_call_target="tpu_custom_call", output_to_operand_aliasing={{1}: (4, {})} | custom-call | tf_op jit(solution)/shard_map/coarse/pallas_call | solution.py:181
  12.9 30.2 %all_to_all.10.x_ref = bf16[16,8,32,256]{3,2,1,0:T(8,128)(2,1)S(1)} all-to-all(bf16[16,8,32,256]{3,2,1,0:T(8,128)(2,1)S(1)} %get-tuple-element.14), channel_id=1, replica_groups=mesh['x'=4,'zh'=4,'zl'=2,'y'=4,'core'=2] {'zl','y','core'}, dimensions={0} | all-to-all | bytes 4194304 | tf_op jit(solution)/shard_map/all_to_all | solution.py:361
  43.1 0.0 copy-done
  43.1 0.0 copy-done.1
  43.1 3.8 %fine.1 = bf16[4,4,32,768]{3,2,1,0:T(8,128)(2,1)S(1)} custom-call(s32[1,256]{1,0:T(1,128)S(1)} %get-tuple-element.10.rate_ref, bf16[16,8,32,256]{3,2,1,0:T(8,128)(2,1)S(1)} %all_to_all.10.x_ref, bf16[512,512]{1,0:T(8,128)(2,1)S(1)} %copy-done, bf16[16,256,256]{2,1,0:T(8,128)(2,1)} %constant.12.clone.second_hbm, bf16[256,256]{1,0:T(8,128)(2,1)S(1)} %copy-done.1), custom_call_target="tpu_custom_call" | custom-call | tf_op jit(solution)/shard_map/fine/pallas_call | solution.py:273
  46.9 35.2 %all_to_all.11.x_ref = bf16[16,32,768]{2,1,0:T(8,128)(2,1)S(1)} all-to-all(bf16[16,32,768]{2,1,0:T(8,128)(2,1)S(1)} %bitcast.2), channel_id=1, replica_groups=mesh['x'=4,'zh'=4,'zl'=2,'y'=4,'core'=2] {'zh','x'}, dimensions={0} | all-to-all | bytes 1572864 | tf_op jit(solution)/shard_map/all_to_all | solution.py:363
  82.1 3.5 %drift.1 = f32[512,512]{1,0:T(8,128)} custom-call(bf16[16,32,768]{2,1,0:T(8,128)(2,1)S(1)} %all_to_all.11.x_ref), custom_call_target="tpu_custom_call" | custom-call | tf_op jit(solution)/shard_map/drift/pallas_call | solution.py:335
  (1 shorter events, 0.0 us)
Async XLA Ops:
  1.0 9.4 %collective-permute-start = (bf16[8,4,4,512]{3,2,1,0:T(4,128)(2,1)S(1)}, bf16[8,4,4,512]{3,2,1,0:T(4,128)(2,1)S(1)}, u32[]{:S(2)}, u32[]{:S(2)}) collective-permute-start(bf16[8,4,4,512]{3,2,1,0:T(4,128)(2,1)S(1)} %slice.3), channel_id=1, source_target_pairs={{1,0},{2,1},{3,2},{4,3},{5,4},{6,5},{7,6},{8,7},{9,8},{10,9},{11,1... | collective-permute-start | bytes 393224 | tf_op jit(solution)/shard_map/ppermute | solution.py:354
  10.4 32.7 %copy-start = (bf16[512,512]{1,0:T(8,128)(2,1)S(1)}, bf16[512,512]{1,0:T(8,128)(2,1)}, u32[]{:S(2)}) copy-start(bf16[512,512]{1,0:T(8,128)(2,1)} %constant.11.clone.first_ref) | copy-start | bytes 1572868
  10.5 32.7 %copy-start.1 = (bf16[256,256]{1,0:T(8,128)(2,1)S(1)}, bf16[256,256]{1,0:T(8,128)(2,1)}, u32[]{:S(2)}) copy-start(bf16[256,256]{1,0:T(8,128)(2,1)} %constant.13.clone.perm_ref) | copy-start | bytes 393220

commit v8 on v7

--- a/solution.py
+++ b/solution.py
@@ -29,7 +29,8 @@
 
 def fine_tables():
     k = np.arange(GRP)
-    ang = (k[:, None] * k[None, :]) % GRP * (2.0 * math.pi / GRP)
+    sent = k % 2 * 8 + k // 2 % 4 * 2 + k // 8
+    ang = (k[:, None] * sent[None, :]) % GRP * (2.0 * math.pi / GRP)
     c, sn = np.cos(ang), np.sin(ang)
     eye = np.eye(16)
     first = np.zeros((GRP, 2, 16, GRP, 2, 16))
@@ -74,7 +75,8 @@
     for r0 in range(0, 256, 16):
         rp = r0 + lax.broadcasted_iota(jnp.int32, (16, N), 0)
         pos = lax.broadcasted_iota(jnp.int32, (16, N), 1)
-        hit = before == (rp // 4) % 4 * 64 + rp // 16 * 4 + rp % 4
+        group = (rp // 16) % 2 * 8 + (rp // 32) % 4 * 2 + rp // 128
+        hit = before == (rp // 4) % 4 * 64 + group * 4 + rp % 4
         hit_ref[r0 : r0 + 16] = hit.astype(f32).astype(bf16)
         chan = jnp.sum(jnp.where(hit, pos, 0), axis=1, keepdims=True)
         cos, sin = cos_sin((chan * pos[:, 0:BLK]) & (N - 1))
@@ -245,7 +247,7 @@
                 pow_ref[2 + 2 * m + h, pl.ds(b, 16, stride=8), :] = tile
     low_lane = lax.broadcasted_iota(jnp.int32, (8, 128), 1)
     step = lax.axis_index(("x", "zh"))
-    own = lax.axis_index(("zl", "y", "core")) * 16
+    own = lax.axis_index(("core", "y", "zl")) * 16
 
     def shift(pair, carry):
         both = []
@@ -358,7 +360,7 @@
     small = jnp.where(row < TAPS, jnp.pad(taps, ((0, 4), (0, 0))), extra)
     wt, rates, tail, filt = front(small, voltages)
     blocks, _ = coarse(tail, halo, small, wt, filt)
-    times = lax.all_to_all(blocks, ("zl", "y", "core"), split_axis=0, concat_axis=0, tiled=True)
+    times = lax.all_to_all(blocks, ("core", "y", "zl"), split_axis=0, concat_axis=0, tiled=True)
     powers = fine(rates, times, jnp.asarray(first), jnp.asarray(second), jnp.asarray(perm))
     wins = lax.all_to_all(powers.reshape(16, 32, WIN), ("zh", "x"), split_axis=0, concat_axis=0, tiled=True)
     out = drift(wins)

time: 85.9 us -> 85.5 us (level)
  no operation moved by 1% of the time
where the time goes in v8:
time: 85.5 us; the launch traced here: 85.3 us
  blocking collectives  65.1 us (76%)
  Pallas kernels  14.4 us (17%)
  starting transfers between devices  3.91 us (5%)
  local copies, waits for them, and re-layouts  1 us (1%)
    all_to_all x1, blocking collectives, shards(): lax.all_to_all(powers.reshape(16, 32, WIN), ('zh', 'x'), split_axis=0, co...  34.9 us
    all_to_all x1, blocking collectives, shards(): lax.all_to_all(blocks, ('core', 'y', 'zl'), split_axis=0, concat_axis=0,...  30.2 us
    pallas_call x1, Pallas kernels, front(): pl.pallas_call(front_kernel, in_specs=[vmem, pl.BlockSpec(memory_space=pl...  4.72 us
    ppermute x1, starting transfers between devices, shards(): halo = lax.ppermute(head, axes, [(i + 1, i) for i in range(devices - 1)])  3.91 us
    pallas_call x1, Pallas kernels, fine(): pl.pallas_call(fine_kernel, in_specs=[pl.BlockSpec(memory_space=pltpu.SME...  3.77 us
    pallas_call x1, Pallas kernels, drift(): pl.pallas_call(drift_kernel, in_specs=[pl.BlockSpec(memory_space=pltpu.VM...  3.46 us
    pallas_call x1, Pallas kernels, coarse(): pl.pallas_call(coarse_kernel, in_specs=[vmem] * 5, out_specs=(vmem, vmem)...  2.41 us
  transfers between devices with their start and end apart: 1, of which 0 were waited for; matrix products, arithmetic and copies ran while one was open for 1% of the time, Pallas kernels for 6%

profile of v8, /device:TPU:32, one launch (start us, length us, event | category | flops | bytes accessed | tf_op | source)
XLA Modules:
  0.0 85.3 jit_solution(271675674912495039)
XLA Ops:
  0.0 1.0 %slice.3 = bf16[8,4,4,512]{3,2,1,0:T(4,128)(2,1)S(1)} slice(bf16[8,4,128,512]{3,2,1,0:T(8,128)(2,1)} %v_ref.1), slice={[0:8], [0:4], [0:4], [0:512]} | slice | bytes 262144 | tf_op jit(solution)/shard_map/slice | solution.py:355
  1.0 3.9 %collective-permute-start = (bf16[8,4,4,512]{3,2,1,0:T(4,128)(2,1)S(1)}, bf16[8,4,4,512]{3,2,1,0:T(4,128)(2,1)S(1)}, u32[]{:S(2)}, u32[]{:S(2)}) collective-permute-start(bf16[8,4,4,512]{3,2,1,0:T(4,128)(2,1)S(1)} %slice.3), channel_id=1, source_target_pairs={{1,0},{2,1},{3,2},{4,3},{5,4},{6,5},{7,6},{8,7},{9,8},{10,9},{11,1... | collective-permute-start | bytes 393224 | tf_op jit(solution)/shard_map/ppermute | solution.py:356
  4.9 0.8 convert_select_fusion.small_ref
  5.7 4.7 %front.1 = (bf16[16,32,1024]{2,1,0:T(8,128)(2,1)S(1)}, s32[1,256]{1,0:T(1,128)S(1)}, bf16[8,4,8,512]{3,2,1,0:T(8,128)(2,1)S(1)}, bf16[8,256,1024]{2,1,0:T(8,128)(2,1)S(1)}) custom-call(f32[8,512]{1,0:T(8,128)S(1)} %convert_select_fusion.small_ref, bf16[8,4,128,512]{3,2,1,0:T(8,128)(2,1)} %v_ref.1), custom_call_target="tpu_custom_call" | custom-call | tf_op jit(solution)/shard_map/front/pallas_call | solution.py:136
  10.4 0.0 collective-permute-done.halo_ref
  10.4 0.0 copy-start
  10.5 0.0 copy-start.1
  10.5 2.4 %coarse.1 = (bf16[16,8,32,256]{3,2,1,0:T(8,128)(2,1)S(1)}, bf16[8,256,1024]{2,1,0:T(8,128)(2,1)S(1)}) custom-call(bf16[8,4,8,512]{3,2,1,0:T(8,128)(2,1)S(1)} %get-tuple-element.11.tail_ref, bf16[8,4,4,512]{3,2,1,0:T(4,128)(2,1)S(1)} %collective-permute-done.halo_ref, f32[8,512]{1,0:T(8,128)S(1)} %convert_select_fusion.small_ref, ...), custom_call_target="tpu_custom_call", output_to_operand_aliasing={{1}: (4, {})} | custom-call | tf_op jit(solution)/shard_map/coarse/pallas_call | solution.py:183
  12.9 30.2 %all_to_all.10.x_ref = bf16[16,8,32,256]{3,2,1,0:T(8,128)(2,1)S(1)} all-to-all(bf16[16,8,32,256]{3,2,1,0:T(8,128)(2,1)S(1)} %get-tuple-element.14), channel_id=1, replica_groups=mesh['x'=4,'zh'=4,'zl'=2,'y'=4,'core'=2] {'core','y','zl'}, dimensions={0} | all-to-all | bytes 4194304 | tf_op jit(solution)/shard_map/all_to_all | solution.py:363
  43.1 0.0 copy-done
  43.1 0.0 copy-done.1
  43.1 3.8 %fine.1 = bf16[4,4,32,768]{3,2,1,0:T(8,128)(2,1)S(1)} custom-call(s32[1,256]{1,0:T(1,128)S(1)} %get-tuple-element.10.rate_ref, bf16[16,8,32,256]{3,2,1,0:T(8,128)(2,1)S(1)} %all_to_all.10.x_ref, bf16[512,512]{1,0:T(8,128)(2,1)S(1)} %copy-done, bf16[16,256,256]{2,1,0:T(8,128)(2,1)} %constant.12.clone.second_hbm, bf16[256,256]{1,0:T(8,128)(2,1)S(1)} %copy-done.1), custom_call_target="tpu_custom_call" | custom-call | tf_op jit(solution)/shard_map/fine/pallas_call | solution.py:275
  46.9 34.9 %all_to_all.11.x_ref = bf16[16,32,768]{2,1,0:T(8,128)(2,1)S(1)} all-to-all(bf16[16,32,768]{2,1,0:T(8,128)(2,1)S(1)} %bitcast.2), channel_id=1, replica_groups=mesh['x'=4,'zh'=4,'zl'=2,'y'=4,'core'=2] {'zh','x'}, dimensions={0} | all-to-all | bytes 1572864 | tf_op jit(solution)/shard_map/all_to_all | solution.py:365
  81.8 3.5 %drift.1 = f32[512,512]{1,0:T(8,128)} custom-call(bf16[16,32,768]{2,1,0:T(8,128)(2,1)S(1)} %all_to_all.11.x_ref), custom_call_target="tpu_custom_call" | custom-call | tf_op jit(solution)/shard_map/drift/pallas_call | solution.py:337
  (1 shorter events, 0.0 us)
Async XLA Ops:
  1.0 9.4 %collective-permute-start = (bf16[8,4,4,512]{3,2,1,0:T(4,128)(2,1)S(1)}, bf16[8,4,4,512]{3,2,1,0:T(4,128)(2,1)S(1)}, u32[]{:S(2)}, u32[]{:S(2)}) collective-permute-start(bf16[8,4,4,512]{3,2,1,0:T(4,128)(2,1)S(1)} %slice.3), channel_id=1, source_target_pairs={{1,0},{2,1},{3,2},{4,3},{5,4},{6,5},{7,6},{8,7},{9,8},{10,9},{11,1... | collective-permute-start | bytes 393224 | tf_op jit(solution)/shard_map/ppermute | solution.py:356
  10.4 32.6 %copy-start = (bf16[512,512]{1,0:T(8,128)(2,1)S(1)}, bf16[512,512]{1,0:T(8,128)(2,1)}, u32[]{:S(2)}) copy-start(bf16[512,512]{1,0:T(8,128)(2,1)} %constant.11.clone.first_ref) | copy-start | bytes 1572868
  10.5 32.6 %copy-start.1 = (bf16[256,256]{1,0:T(8,128)(2,1)S(1)}, bf16[256,256]{1,0:T(8,128)(2,1)}, u32[]{:S(2)}) copy-start(bf16[256,256]{1,0:T(8,128)(2,1)} %constant.13.clone.perm_ref) | copy-start | bytes 393220
